TPU v7x, 256 devices: a whole 4x4x8 slice. The times are simulated.
256 devices in a mesh: mem: 64 (over x, z, core), chan: 4 (over y).
Axes of the slice: x: 4, y: 4, z: 8, core: 2. Of those that a mesh axis runs over, the one named last changes fastest.
Arguments:
- state_anom: bfloat16 [64, 512, 137], P(None, 'mem'), may hold values from -6 to 6
- radiance_anom: bfloat16 [64, 512, 8704], P(None, 'mem', 'chan'), may hold values from -6 to 6
- inv_noise: float32 [8704], P('chan'), may hold values from 0.02 to 0.2
- innovation: float32 [64, 8704], P(None, 'chan'), may hold values from -6 to 6
- valid_count: int32 [64], replicated, may hold values from 4352 to 8461
Outputs:
- information: float32 [64, 137, 137], P('mem')
- gradient: float32 [64, 137], P('mem')
- increment: float32 [64, 137], P('mem')
All inputs are finite; a program needn't handle non-finite values.
Results may differ from a plain program's by a relative error of at most 0.0003.
Values may be sent and summed in bfloat16 or wider, within the bound.
No kernel may reach another device: no remote copies, remote signals or barrier semaphores. Data moves between devices by JAX's collectives and lax.ppermute only.
A program may use at most 64 MiB of HBM per device.

v0:
```python
import functools

import jax
import jax.numpy as jnp
from jax import lax
from jax.experimental import pallas as pl
from jax.experimental.pallas import tpu as pltpu
from jax.sharding import PartitionSpec as P

LANES = 128
TOL = 2e-5
FIRST_STEPS = 11
MORE_STEPS = 6
MORE_ROUNDS = 8
PACKED = 96


def places(rows):
    r = lax.broadcasted_iota(jnp.int32, (rows, LANES), 0)
    c = lax.broadcasted_iota(jnp.int32, (rows, LANES), 1)
    return r, c


SIZE_X, SIZE_Z, SIZE_C = 4, 8, 2
ACROSS = ((0, 0), (2, 0), (2, 1), (1, 0), (3, 0), (1, 1), (3, 1), (0, 1))
NEAR = (2, -2, 1, -1, 0)
FAR = (4, 3, -3)
SENT = len(NEAR) - 1 + len(ACROSS) - 1


def partner(x, z, c):
    return (x % SIZE_X * SIZE_Z + z % SIZE_Z) * SIZE_C + c % SIZE_C


def slot_of(me, dx, dz, dc):
    x, z, c = me // (SIZE_Z * SIZE_C), me // SIZE_C % SIZE_Z, me % SIZE_C
    across = lax.rem(x + dx, SIZE_X) * (SIZE_Z * SIZE_C) + lax.rem(c + dc, SIZE_C)
    return across + lax.rem(z + dz + SIZE_Z, SIZE_Z) * SIZE_C


def spread_kernel(rad_ref, st_ref, *refs):
    outs, own, held, (st, arrived, left) = refs[:SENT], refs[SENT : SENT + 2], refs[SENT + 2 : -3], refs[-3:]
    width = rad_ref.shape[2]
    states = st_ref.shape[2]
    me = lax.axis_index("mem")
    first = pltpu.make_async_copy(st_ref, st, arrived.at[SIZE_X * SIZE_Z * SIZE_C])
    first.start()
    near = held[: len(NEAR) - 1] + own[:1]
    far = own[1:] + held[len(NEAR) - 1 :]
    groups = [(near[i], [(k, dz, o) for k, o in enumerate(ACROSS)]) for i, dz in enumerate(NEAR)]
    groups += [(far[i], [(k, dz, o) for k, dz in enumerate(FAR)]) for i, o in enumerate(ACROSS)]
    groups.sort(key=lambda group: any(group[0] is ref for ref in own))
    copies, count = [], 0
    for ref, slots in groups:
        copies.append([])
        for k, dz, (dx, dc) in slots:
            p = slot_of(me, dx, dz, dc)
            copy = pltpu.make_async_copy(rad_ref.at[p], ref.at[k, :, pl.ds(0, width)], arrived.at[count])
            copy.start()
            copies[-1].append((copy, k, p))
            count += 1
    first.wait()
    for (ref, _), group in zip(groups, copies):
        for _, k, p in group if any(ref is each for each in near) else ():
            ref[k, :, width : width + states] = st[p]
    away = []
    for (ref, _), group in zip(groups, copies):
        for copy, _, _ in group:
            copy.wait()
        for i, source in enumerate(held):
            if source is ref:
                away.append(pltpu.make_async_copy(ref, outs[i], left.at[i]))
                away[-1].start()
    for copy in away:
        copy.wait()


def pack_kernel(st_ref, *outs):
    me = lax.axis_index("mem")
    for dz, out in zip(FAR, outs):
        ends = []
        for o, (dx, dc) in enumerate(ACROSS):
            p = slot_of(me, dx, dz, dc)
            out[o] = st_ref[p, :, 0:LANES]
            ends.append(st_ref[p, :, LANES:].astype(jnp.float32))
        rest = st_ref.shape[2] - LANES
        ends.append(jnp.zeros((ends[0].shape[0], LANES - rest * len(ACROSS)), jnp.float32))
        out[len(ACROSS)] = jnp.concatenate(ends, axis=1).astype(out.dtype)


def swap_kernel(many, *refs):
    come, go = refs[:many], refs[many:]
    for i, ref in enumerate(come):
        for j, out in enumerate(go):
            out[i] = ref[j]


def swap_both_kernel(states, *refs):
    near, packed, outs = refs[: len(NEAR)], refs[len(NEAR) : len(NEAR) + len(FAR)], refs[len(NEAR) + len(FAR) :]
    base = near[0].shape[2]
    rest = states - LANES
    for i, ref in enumerate(near):
        for o, out in enumerate(outs):
            out[i, :, 0:base] = ref[o]
    for d, ref in enumerate(packed):
        ends = ref[len(outs)].astype(jnp.float32)
        for o, out in enumerate(outs):
            out[d, :, base : base + LANES] = ref[o]
            out[d, :, base + LANES : base + states] = ends[:, o * rest : (o + 1) * rest].astype(out.dtype)


def in_vmem(kernel, outs, count, **more):
    return pl.pallas_call(
        kernel,
        out_shape=outs,
        in_specs=[pl.BlockSpec(memory_space=pltpu.VMEM)] * count,
        out_specs=[pl.BlockSpec(memory_space=pltpu.VMEM)] * len(outs),
        compiler_params=pltpu.CompilerParams(vmem_limit_bytes=20 * 2**20),
        **more,
    )


def moved(a, dx, dz, dc):
    pairs = [
        (partner(x, z, c), partner(x + dx, z + dz, c + dc))
        for x in range(SIZE_X)
        for z in range(SIZE_Z)
        for c in range(SIZE_C)
    ]
    return lax.ppermute(a, "mem", pairs)


def gathered(rad, st):
    members, width = rad.shape[1], rad.shape[2]
    wide = width + 2 * LANES
    shape = lambda rows, lanes: [jax.ShapeDtypeStruct((rows, members, lanes), rad.dtype)]
    tall = shape(len(ACROSS), width)
    flat = shape(len(FAR), width)
    sent = shape(len(ACROSS), wide) * (len(NEAR) - 1) + flat * (len(ACROSS) - 1)
    spread = pl.pallas_call(
        spread_kernel,
        out_shape=sent + [pltpu.VMEM(a.shape, a.dtype) for a in shape(len(ACROSS), wide) + flat],
        in_specs=[pl.BlockSpec(memory_space=pltpu.HBM)] * 2,
        out_specs=[pl.BlockSpec(memory_space=pltpu.HBM)] * SENT + [pl.BlockSpec(memory_space=pltpu.VMEM)] * 2,
        scratch_shapes=[pltpu.VMEM(a.shape, a.dtype) for a in sent]
        + [
            pltpu.VMEM(st.shape, st.dtype),
            pltpu.SemaphoreType.DMA((st.shape[0] + 1,)),
            pltpu.SemaphoreType.DMA((SENT,)),
        ],
        compiler_params=pltpu.CompilerParams(vmem_limit_bytes=59 * 10**6),
        name="spread",
    )(rad, st)
    near = spread[: len(NEAR) - 1] + spread[SENT : SENT + 1]
    far = spread[SENT + 1 :] + spread[len(NEAR) - 1 : SENT]
    near = [a if dz == 0 else moved(a, 0, dz, 0) for a, dz in zip(near, NEAR)]
    far = [a if o == (0, 0) else moved(a, o[0], 0, o[1]) for a, o in zip(far, ACROSS)]
    packed = in_vmem(pack_kernel, shape(len(ACROSS) + 1, LANES) * len(FAR), 1)(st)
    packed = [moved(a, 0, dz, 0) for a, dz in zip(packed, FAR)]
    far = in_vmem(functools.partial(swap_kernel, len(ACROSS)), tall * len(FAR), len(ACROSS))(*far)
    far = [moved(a, 0, dz, 0) for a, dz in zip(far, FAR)]
    both = shape(len(NEAR), wide + 2 * LANES) * len(ACROSS)
    swap_both = in_vmem(functools.partial(swap_both_kernel, st.shape[2]), both, len(NEAR) + len(FAR))
    near = swap_both(*near, *packed)
    near = [a if o == (0, 0) else moved(a, o[0], 0, o[1]) for a, o in zip(near, ACROSS)]
    return far + near


def slab_kernel(states, members_all, *refs):
    parts, (weight_ref, innov_ref, out_ref, x_ref) = refs[:-4], refs[-4:]
    width = weight_ref.shape[1]
    far, near = parts[: len(FAR)], parts[len(FAR) :]
    members = far[0].shape[1]
    block = members * len(NEAR)
    above = members * len(ACROSS) * len(FAR)
    for k, part in enumerate(far):
        x_ref[k * members * len(ACROSS) : (k + 1) * members * len(ACROSS), 0:width] = part[...].reshape(-1, width)
    for o, part in enumerate(near):
        x_ref[above + o * block : above + (o + 1) * block, :] = part[:, :, 0 : x_ref.shape[1]].reshape(block, -1)
        for k in range(len(FAR)):
            row = (k * len(ACROSS) + o) * members
            base = width + 2 * LANES
            x_ref[row : row + members, width : width + states] = part[k, :, base : base + states]
    rad = x_ref[:, 0:width]
    st = x_ref[:, width : width + states]
    cross = lax.dot_general(st, rad, (((0,), (0,)), ((), ())), preferred_element_type=jnp.float32)
    root = jnp.sqrt(weight_ref[...])
    y = cross * (root * (1.0 / (members_all - 1)))
    y1 = y.astype(jnp.bfloat16)
    y2 = (y - y1.astype(jnp.float32)).astype(jnp.bfloat16)
    nt = (((1,), (1,)), ((), ()))
    main = lax.dot_general(y1, y1, nt, preferred_element_type=jnp.float32)
    side = lax.dot_general(y2, y1, nt, preferred_element_type=jnp.float32)
    info = main + (side + side.T)
    grad = jnp.sum(y * (root * innov_ref[...]), axis=1, keepdims=True)
    r = lax.broadcasted_iota(jnp.int32, info.shape, 0)
    c = lax.broadcasted_iota(jnp.int32, info.shape, 1)
    grad_row = jnp.sum(jnp.where(r == c, grad, 0.0), axis=0, keepdims=True)
    rest = states - LANES
    half = LANES // 2
    other = pltpu.roll(info[half:LANES, 0:LANES], half, 1)
    r, c = places(half)
    out_ref[0:half, :] = jnp.where(c < r, other, info[0:half, 0:LANES])
    out_ref[half:, :] = jnp.zeros((PACKED - half, LANES), jnp.float32)
    out_ref[half : half + rest, :] = info[LANES:states, 0:LANES]
    out_ref[half + rest : half + rest + 1, :] = grad_row[:, 0:LANES]
    out_ref[half + rest + 1 : half + rest + 2, :] = jnp.sum(jnp.where(r == c, other, 0.0), axis=0, keepdims=True)
    out_ref[half + 16 : half + 16 + rest, 0:rest] = info[LANES:states, LANES:states]
    out_ref[half + 16 + rest : half + 17 + rest, 0:rest] = grad_row[:, LANES:states]


def solve_kernel(
    states, a_ref, b_ref, c_ref, d_ref, info_ref, grad_ref, inc_ref, info, grad, inc, left, right, x_ref, r_ref, gj, done
):
    rest = states - LANES
    rows = LANES + 16
    half = LANES // 2
    total = (a_ref[...] + b_ref[...]) + (c_ref[...] + d_ref[...])
    r, c = places(half)
    ra, ca = places(LANES)
    last = jnp.where(ca[0:1] < half, total[half + rest + 1 : half + rest + 2, :], 0.0)
    lower = jnp.where(c < r, total[0:half], 0.0) + jnp.where(c == r, last, 0.0)
    part = jnp.concatenate([jnp.where(c < r, 0.0, total[0:half]), pltpu.roll(lower, half, 1)], axis=0)
    square = jnp.where(ra == ca, part, part + part.T)
    r, c = places(16)
    low = jnp.where(r < rest, total[half : half + 16, :], 0.0)
    corner = jnp.where((r < rest) & (c < rest), total[half + 16 : half + 32, :], 0.0)
    g0 = total[half + rest : half + rest + 1, :]
    g1 = total[half + 16 + rest : half + 17 + rest, :]
    upper = jnp.concatenate([low, jnp.zeros((LANES - 16, LANES), jnp.float32)], axis=0).T
    info[:, 0, 0:LANES] = jnp.concatenate([square, low[0:rest]], axis=0)
    info[:, 0, LANES:states] = jnp.concatenate([upper[:, 0:rest], corner[0:rest, 0:rest]], axis=0)
    grad[:, 0:LANES] = g0
    grad[:, LANES:states] = g1[:, 0:rest]
    eye = (ra == ca).astype(jnp.float32)
    eye_low = (r == c).astype(jnp.float32)
    left[0:LANES, :] = square + eye
    left[LANES:rows, :] = low
    right[0:LANES, :] = upper
    right[LANES:rows, :] = corner + eye_low
    early = (
        pltpu.make_async_copy(info, info_ref, done.at[0]),
        pltpu.make_async_copy(grad, grad_ref, done.at[1]),
    )
    for copy in early:
        copy.start()

    def to_rows(v):
        return (
            jnp.sum(v[0:LANES] * eye, axis=0, keepdims=True),
            jnp.sum(v[LANES:rows] * eye_low, axis=0, keepdims=True),
        )

    def times(v):
        v0, v1 = to_rows(v)
        return jnp.broadcast_to(jnp.sum(left[...] * v0 + right[...] * v1, axis=1, keepdims=True), (rows, LANES))

    def dot(u, v):
        return jnp.sum(u * v, axis=0, keepdims=True)

    def ratio(num, den):
        return jnp.where(den > 0.0, num / jnp.where(den > 0.0, den, 1.0), 0.0)

    def steps(n, x, res, p, s, gamma, alpha):
        for _ in range(n):
            w = times(res)
            new = dot(res, res)
            delta = dot(res, w)
            if gamma is None:
                alpha = ratio(new, delta)
                p, s = res, w
            else:
                beta = ratio(new, gamma)
                alpha = ratio(new, delta - beta * ratio(new, alpha))
                p = res + beta * p
                s = w + beta * s
            x = x + alpha * p
            res = res - alpha * s
            gamma = new
        return x, res

    col = jnp.concatenate(
        [
            jnp.broadcast_to(jnp.sum(eye * g0, axis=1, keepdims=True), (LANES, LANES)),
            jnp.broadcast_to(jnp.sum(jnp.where(c < rest, eye_low * g1, 0.0), axis=1, keepdims=True), (16, LANES)),
        ],
        axis=0,
    )

    def put(x):
        x0, x1 = to_rows(x)
        inc[:, 0:LANES] = x0
        inc[:, LANES:states] = x1[:, 0:rest]

    def open_after(x):
        res = col - times(x)
        bad = jnp.logical_not(dot(res, res) <= (TOL * TOL) * dot(x, x))
        return jnp.max(bad[:, 0:1].astype(jnp.int32)), res

    x, _ = steps(FIRST_STEPS, jnp.zeros_like(col), col, None, None, None, None)
    put(x)
    still, res = open_after(x)

    @pl.when(still > 0)
    def _():
        x_ref[...] = x
        r_ref[...] = res

        def more(state):
            k, _ = state
            x, _ = steps(MORE_STEPS, x_ref[...], r_ref[...], None, None, None, None)
            still, res = open_after(x)
            x_ref[...] = x
            r_ref[...] = res
            return k + 1, still

        _, open_still = lax.while_loop(
            lambda s: (s[0] < MORE_ROUNDS) & (s[1] > 0), more, (jnp.int32(0), jnp.int32(1))
        )
        put(x_ref[...])

        @pl.when(open_still > 0)
        def _():
            wide_r = lax.broadcasted_iota(jnp.int32, (rows, 3 * LANES), 0)
            wide_c = lax.broadcasted_iota(jnp.int32, (rows, 3 * LANES), 1)
            gj[:, 0:LANES] = left[...]
            gj[:, LANES : 2 * LANES] = right[...]
            gj[:, 2 * LANES : 3 * LANES] = col

            def eliminate(i, _):
                a = gj[...]
                row = jnp.sum(jnp.where(wide_r == i, a, 0.0), axis=0, keepdims=True)
                lane = lax.broadcasted_iota(jnp.int32, row.shape, 1)
                pivot = jnp.sum(jnp.where(lane == i, row, 0.0), axis=1, keepdims=True)
                row = row / pivot
                column = jnp.sum(jnp.where(wide_c == i, a, 0.0), axis=1, keepdims=True)
                gj[...] = jnp.where(wide_r == i, row, a - column * row)
                return 0

            lax.fori_loop(0, states, eliminate, 0)
            put(gj[:, 2 * LANES : 3 * LANES])

    late = pltpu.make_async_copy(inc, inc_ref, done.at[2])
    late.start()
    for copy in early:
        copy.wait()
    late.wait()


def shards(state_anom, radiance_anom, inv_noise, innovation, valid_count):
    _, local_members, states = state_anom.shape
    slab_width = radiance_anom.shape[2]
    mem = lax.axis_size("mem")
    chan = lax.axis_size("chan")
    members_all = local_members * mem
    f32 = jnp.float32
    blocks = gathered(radiance_anom, state_anom)
    prof = lax.axis_index("mem")
    own_count = lax.dynamic_slice_in_dim(valid_count, prof, 1, 0)
    slots = lax.axis_index("chan") * slab_width + jnp.arange(slab_width, dtype=jnp.int32)
    weight = jnp.where(slots[None, :] < own_count[:, None], inv_noise[None, :], 0.0)
    innov = lax.dynamic_slice_in_dim(innovation, prof, 1, 0)
    part = pl.pallas_call(
        functools.partial(slab_kernel, states, members_all),
        out_shape=jax.ShapeDtypeStruct((PACKED, LANES), f32),
        in_specs=[pl.BlockSpec(memory_space=pltpu.VMEM)] * (len(blocks) + 2),
        out_specs=pl.BlockSpec(memory_space=pltpu.VMEM),
        scratch_shapes=[pltpu.VMEM((members_all, slab_width + 2 * LANES), jnp.bfloat16)],
        compiler_params=pltpu.CompilerParams(vmem_limit_bytes=24 * 2**20),
        name="slab",
    )(*blocks, weight, innov)
    parts = [part] + [
        lax.ppermute(part, "chan", [(j, (j + k) % chan) for j in range(chan)]) for k in (2, 1, 3)
    ]
    outs = [(states, 1, states), (1, states), (1, states)]
    square = pltpu.VMEM((LANES + 16, LANES), f32)
    info, grad, inc = pl.pallas_call(
        functools.partial(solve_kernel, states),
        out_shape=[jax.ShapeDtypeStruct(shape, f32) for shape in outs],
        in_specs=[pl.BlockSpec(memory_space=pltpu.VMEM)] * 4,
        out_specs=[pl.BlockSpec(memory_space=pltpu.HBM)] * 3,
        scratch_shapes=[pltpu.VMEM(shape, f32) for shape in outs]
        + [square] * 4
        + [pltpu.VMEM((LANES + 16, 3 * LANES), f32), pltpu.SemaphoreType.DMA((3,))],
        compiler_params=pltpu.CompilerParams(vmem_limit_bytes=8 * 2**20),
        name="solve",
    )(*parts)
    return (jnp.transpose(info, (1, 0, 2)), grad, inc)


def solution(mesh):
    in_specs = (P(None, "mem", None), P(None, "mem", "chan"), P("chan"), P(None, "chan"), P())
    out_specs = (P("mem", None, None), P("mem", None), P("mem", None))
    return jax.shard_map(shards, mesh=mesh, in_specs=in_specs, out_specs=out_specs, check_vma=False)
```

profile of v0, /device:TPU:1, one launch (start us, length us, event | category | flops | bytes accessed | tf_op | source)
XLA Modules:
  0.0 113.3 jit_solution(16276440678837300504)
XLA Ops:
  0.7 3.0 %spread.1 = (bf16[8,8,2432]{2,1,0:T(8,128)(2,1)}, bf16[8,8,2432]{2,1,0:T(8,128)(2,1)}, bf16[8,8,2432]{2,1,0:T(8,128)(2,1)}, bf16[8,8,2432]{2,1,0:T(8,128)(2,1)},...) custom-call(bf16[64,8,2176]{2,1,0:T(8,128)(2,1)} %rad_ref.1, ...), custom_call_target="tpu_custom_call" | custom-call | tf_op jit(solution)/shard_map/spread/pallas_call | solution.py:140
  3.7 3.6 %collective-permute-start = (bf16[3,8,2176]{2,1,0:T(8,128)(2,1)}, bf16[3,8,2176]{2,1,0:T(8,128)(2,1)S(1)}, u32[]{:S(2)}, u32[]{:S(2)}) collective-permute-start(bf16[3,8,2176]{2,1,0:T(8,128)(2,1)} %get-tuple-element.34), channel_id=1, source_target_pairs={{0,128},{4,132},{8,136},{12,140},{16,144},{20,148},{24,152},{28,15... | collective-permute-start | bytes 313352 | tf_op jit(solution)/shard_map/ppermute | solution.py:130
  7.3 2.8 %collective-permute-start.1 = (bf16[3,8,2176]{2,1,0:T(8,128)(2,1)}, bf16[3,8,2176]{2,1,0:T(8,128)(2,1)S(1)}, u32[]{:S(2)}, u32[]{:S(2)}) collective-permute-start(bf16[3,8,2176]{2,1,0:T(8,128)(2,1)} %get-tuple-element.35), channel_id=1, source_target_pairs={{0,132},{4,128},{8,140},{12,136},{16,148},{20,144},{24,156},{28,15... | collective-permute-start | bytes 313352 | tf_op jit(solution)/shard_map/ppermute | solution.py:130
  10.2 5.3 %collective-permute-start.14 = (bf16[9,8,128]{2,1,0:T(8,128)(2,1)S(1)}, bf16[9,8,128]{2,1,0:T(8,128)(2,1)S(1)}, u32[]{:S(2)}, u32[]{:S(2)}) collective-permute-start(bf16[9,8,128]{2,1,0:T(8,128)(2,1)S(1)} %get-tuple-element.49), channel_id=1, source_target_pairs={{0,32},{4,36},{8,40},{12,44},{16,48},{20,52},{24,56},{28,60},{32,0... | collective-permute-start | bytes 55304 | tf_op jit(solution)/shard_map/ppermute | solution.py:130
  15.5 1.2 %collective-permute-start.2 = (bf16[3,8,2176]{2,1,0:T(8,128)(2,1)}, bf16[3,8,2176]{2,1,0:T(8,128)(2,1)S(1)}, u32[]{:S(2)}, u32[]{:S(2)}) collective-permute-start(bf16[3,8,2176]{2,1,0:T(8,128)(2,1)} %get-tuple-element.36), channel_id=1, source_target_pairs={{0,64},{4,68},{8,72},{12,76},{16,80},{20,84},{24,88},{28,92},{32,9... | collective-permute-start | bytes 313352 | tf_op jit(solution)/shard_map/ppermute | solution.py:130
  16.7 1.5 %collective-permute-start.3 = (bf16[3,8,2176]{2,1,0:T(8,128)(2,1)}, bf16[3,8,2176]{2,1,0:T(8,128)(2,1)S(1)}, u32[]{:S(2)}, u32[]{:S(2)}) collective-permute-start(bf16[3,8,2176]{2,1,0:T(8,128)(2,1)} %get-tuple-element.37), channel_id=1, source_target_pairs={{0,192},{4,196},{8,200},{12,204},{16,208},{20,212},{24,216},{28,22... | collective-permute-start | bytes 313352 | tf_op jit(solution)/shard_map/ppermute | solution.py:130
  18.2 1.6 %collective-permute-start.15 = (bf16[9,8,128]{2,1,0:T(8,128)(2,1)S(1)}, bf16[9,8,128]{2,1,0:T(8,128)(2,1)S(1)}, u32[]{:S(2)}, u32[]{:S(2)}) collective-permute-start(bf16[9,8,128]{2,1,0:T(8,128)(2,1)S(1)} %get-tuple-element.50), channel_id=1, source_target_pairs={{0,24},{4,28},{8,32},{12,36},{16,40},{20,44},{24,48},{28,52},{32,5... | collective-permute-start | bytes 55304 | tf_op jit(solution)/shard_map/ppermute | solution.py:130
  19.8 4.0 %collective-permute-done.15.refs_6_ = bf16[9,8,128]{2,1,0:T(8,128)(2,1)S(1)} collective-permute-done((bf16[9,8,128]{2,1,0:T(8,128)(2,1)S(1)}, bf16[9,8,128]{2,1,0:T(8,128)(2,1)S(1)}, u32[]{:S(2)}, u32[]{:S(2)}) %collective-permute-start.15) | collective-permute-done | bytes 18464 | tf_op jit(solution)/shard_map/ppermute | solution.py:130
  23.8 1.8 %collective-permute-start.4 = (bf16[3,8,2176]{2,1,0:T(8,128)(2,1)}, bf16[3,8,2176]{2,1,0:T(8,128)(2,1)S(1)}, u32[]{:S(2)}, u32[]{:S(2)}) collective-permute-start(bf16[3,8,2176]{2,1,0:T(8,128)(2,1)} %get-tuple-element.38), channel_id=1, source_target_pairs={{0,68},{4,64},{8,76},{12,72},{16,84},{20,80},{24,92},{28,88},{32,1... | collective-permute-start | bytes 313352 | tf_op jit(solution)/shard_map/ppermute | solution.py:130
  25.6 1.3 %collective-permute-start.10 = (bf16[8,8,2432]{2,1,0:T(8,128)(2,1)}, bf16[8,8,2432]{2,1,0:T(8,128)(2,1)S(1)}, u32[]{:S(2)}, u32[]{:S(2)}) collective-permute-start(bf16[8,8,2432]{2,1,0:T(8,128)(2,1)} %get-tuple-element.44), channel_id=1, source_target_pairs={{0,16},{4,20},{8,24},{12,28},{16,32},{20,36},{24,40},{28,44},{32,4... | collective-permute-start | bytes 933896 | tf_op jit(solution)/shard_map/ppermute | solution.py:130
  26.9 3.1 %collective-permute-start.11 = (bf16[8,8,2432]{2,1,0:T(8,128)(2,1)}, bf16[8,8,2432]{2,1,0:T(8,128)(2,1)S(1)}, u32[]{:S(2)}, u32[]{:S(2)}) collective-permute-start(bf16[8,8,2432]{2,1,0:T(8,128)(2,1)} %get-tuple-element.45), channel_id=1, source_target_pairs={{0,48},{4,52},{8,56},{12,60},{16,0},{20,4},{24,8},{28,12},{32,16},... | collective-permute-start | bytes 933896 | tf_op jit(solution)/shard_map/ppermute | solution.py:130
  30.0 2.7 %collective-permute-start.13 = (bf16[8,8,2432]{2,1,0:T(8,128)(2,1)}, bf16[8,8,2432]{2,1,0:T(8,128)(2,1)S(1)}, u32[]{:S(2)}, u32[]{:S(2)}) collective-permute-start(bf16[8,8,2432]{2,1,0:T(8,128)(2,1)} %get-tuple-element.47), channel_id=1, source_target_pairs={{0,56},{4,60},{8,0},{12,4},{16,8},{20,12},{24,16},{28,20},{32,24},... | collective-permute-start | bytes 933896 | tf_op jit(solution)/shard_map/ppermute | solution.py:130
  32.7 2.1 %collective-permute-start.5 = (bf16[3,8,2176]{2,1,0:T(8,128)(2,1)}, bf16[3,8,2176]{2,1,0:T(8,128)(2,1)S(1)}, u32[]{:S(2)}, u32[]{:S(2)}) collective-permute-start(bf16[3,8,2176]{2,1,0:T(8,128)(2,1)} %get-tuple-element.39), channel_id=1, source_target_pairs={{0,196},{4,192},{8,204},{12,200},{16,212},{20,208},{24,220},{28,21... | collective-permute-start | bytes 313352 | tf_op jit(solution)/shard_map/ppermute | solution.py:130
  34.8 3.3 %collective-permute-done.5.refs_6_ = bf16[3,8,2176]{2,1,0:T(8,128)(2,1)S(1)} collective-permute-done((bf16[3,8,2176]{2,1,0:T(8,128)(2,1)}, bf16[3,8,2176]{2,1,0:T(8,128)(2,1)S(1)}, u32[]{:S(2)}, u32[]{:S(2)}) %collective-permute-start.5) | collective-permute-done | bytes 104480 | tf_op jit(solution)/shard_map/ppermute | solution.py:130
  38.3 1.4 %collective-permute-done.6.refs_7_ = bf16[3,8,2176]{2,1,0:T(8,128)(2,1)S(1)} collective-permute-done((bf16[3,8,2176]{2,1,0:T(8,128)(2,1)}, bf16[3,8,2176]{2,1,0:T(8,128)(2,1)S(1)}, u32[]{:S(2)}, u32[]{:S(2)}) %collective-permute-start.6) | collective-permute-done | bytes 104480 | tf_op jit(solution)/shard_map/ppermute | solution.py:130
  39.7 2.9 %collective-permute-start.16 = (bf16[9,8,128]{2,1,0:T(8,128)(2,1)S(1)}, bf16[9,8,128]{2,1,0:T(8,128)(2,1)S(1)}, u32[]{:S(2)}, u32[]{:S(2)}) collective-permute-start(bf16[9,8,128]{2,1,0:T(8,128)(2,1)S(1)} %get-tuple-element.51), channel_id=1, source_target_pairs={{0,40},{4,44},{8,48},{12,52},{16,56},{20,60},{24,0},{28,4},{32,8},... | collective-permute-start | bytes 55304 | tf_op jit(solution)/shard_map/ppermute | solution.py:130
  43.4 9.3 %collective-permute-done.16.refs_7_ = bf16[9,8,128]{2,1,0:T(8,128)(2,1)S(1)} collective-permute-done((bf16[9,8,128]{2,1,0:T(8,128)(2,1)S(1)}, bf16[9,8,128]{2,1,0:T(8,128)(2,1)S(1)}, u32[]{:S(2)}, u32[]{:S(2)}) %collective-permute-start.16) | collective-permute-done | bytes 18464 | tf_op jit(solution)/shard_map/ppermute | solution.py:130
  52.8 3.1 %collective-permute-start.7 = (bf16[8,8,2176]{2,1,0:T(8,128)(2,1)}, bf16[8,8,2176]{2,1,0:T(8,128)(2,1)S(1)}, u32[]{:S(2)}, u32[]{:S(2)}) collective-permute-start(bf16[8,8,2176]{2,1,0:T(8,128)(2,1)} %get-tuple-element.41), channel_id=1, source_target_pairs={{0,32},{4,36},{8,40},{12,44},{16,48},{20,52},{24,56},{28,60},{32,0... | collective-permute-start | bytes 835592 | tf_op jit(solution)/shard_map/ppermute | solution.py:130
  55.9 2.3 %collective-permute-start.8 = (bf16[8,8,2176]{2,1,0:T(8,128)(2,1)}, bf16[8,8,2176]{2,1,0:T(8,128)(2,1)S(1)}, u32[]{:S(2)}, u32[]{:S(2)}) collective-permute-start(bf16[8,8,2176]{2,1,0:T(8,128)(2,1)} %get-tuple-element.42), channel_id=1, source_target_pairs={{0,24},{4,28},{8,32},{12,36},{16,40},{20,44},{24,48},{28,52},{32,5... | collective-permute-start | bytes 835592 | tf_op jit(solution)/shard_map/ppermute | solution.py:130
  58.2 3.2 %collective-permute-start.9 = (bf16[8,8,2176]{2,1,0:T(8,128)(2,1)S(1)}, bf16[8,8,2176]{2,1,0:T(8,128)(2,1)S(1)}, u32[]{:S(2)}, u32[]{:S(2)}) collective-permute-start(bf16[8,8,2176]{2,1,0:T(8,128)(2,1)S(1)} %get-tuple-element.43), channel_id=1, source_target_pairs={{0,40},{4,44},{8,48},{12,52},{16,56},{20,60},{24,0},{28,4},{32,8},... | collective-permute-start | bytes 835592 | tf_op jit(solution)/shard_map/ppermute | solution.py:130
  62.1 2.4 %collective-permute-start.17 = (bf16[5,8,2688]{2,1,0:T(8,128)(2,1)S(1)}, bf16[5,8,2688]{2,1,0:T(8,128)(2,1)S(1)}, u32[]{:S(2)}, u32[]{:S(2)}) collective-permute-start(bf16[5,8,2688]{2,1,0:T(8,128)(2,1)S(1)} %get-tuple-element.53), channel_id=1, source_target_pairs={{0,128},{4,132},{8,136},{12,140},{16,144},{20,148},{24,152},{28,15... | collective-permute-start | bytes 645128 | tf_op jit(solution)/shard_map/ppermute | solution.py:130
  64.6 1.8 %collective-permute-start.18 = (bf16[5,8,2688]{2,1,0:T(8,128)(2,1)S(1)}, bf16[5,8,2688]{2,1,0:T(8,128)(2,1)S(1)}, u32[]{:S(2)}, u32[]{:S(2)}) collective-permute-start(bf16[5,8,2688]{2,1,0:T(8,128)(2,1)S(1)} %get-tuple-element.54), channel_id=1, source_target_pairs={{0,132},{4,128},{8,140},{12,136},{16,148},{20,144},{24,156},{28,15... | collective-permute-start | bytes 645128 | tf_op jit(solution)/shard_map/ppermute | solution.py:130
  68.0 20.5 %collective-permute-done.8.refs_1_ = bf16[8,8,2176]{2,1,0:T(8,128)(2,1)S(1)} collective-permute-done((bf16[8,8,2176]{2,1,0:T(8,128)(2,1)}, bf16[8,8,2176]{2,1,0:T(8,128)(2,1)S(1)}, u32[]{:S(2)}, u32[]{:S(2)}) %collective-permute-start.8) | collective-permute-done | bytes 278560 | tf_op jit(solution)/shard_map/ppermute | solution.py:130
  88.6 1.6 %collective-permute-start.20 = (bf16[5,8,2688]{2,1,0:T(8,128)(2,1)S(1)}, bf16[5,8,2688]{2,1,0:T(8,128)(2,1)S(1)}, u32[]{:S(2)}, u32[]{:S(2)}) collective-permute-start(bf16[5,8,2688]{2,1,0:T(8,128)(2,1)S(1)} %get-tuple-element.56), channel_id=1, source_target_pairs={{0,192},{4,196},{8,200},{12,204},{16,208},{20,212},{24,216},{28,22... | collective-permute-start | bytes 645128 | tf_op jit(solution)/shard_map/ppermute | solution.py:130
  90.8 2.3 %collective-permute-start.22 = (bf16[5,8,2688]{2,1,0:T(8,128)(2,1)S(1)}, bf16[5,8,2688]{2,1,0:T(8,128)(2,1)S(1)}, u32[]{:S(2)}, u32[]{:S(2)}) collective-permute-start(bf16[5,8,2688]{2,1,0:T(8,128)(2,1)S(1)} %get-tuple-element.58), channel_id=1, source_target_pairs={{0,196},{4,192},{8,204},{12,200},{16,212},{20,208},{24,220},{28,21... | collective-permute-start | bytes 645128 | tf_op jit(solution)/shard_map/ppermute | solution.py:130
  94.8 4.3 %collective-permute-done.21.refs_8_ = bf16[5,8,2688]{2,1,0:T(8,128)(2,1)S(1)} collective-permute-done((bf16[5,8,2688]{2,1,0:T(8,128)(2,1)S(1)}, bf16[5,8,2688]{2,1,0:T(8,128)(2,1)S(1)}, u32[]{:S(2)}, u32[]{:S(2)}) %collective-permute-start.21) | collective-permute-done | bytes 215072 | tf_op jit(solution)/shard_map/ppermute | solution.py:130
  99.1 1.1 collective-permute-done.22.refs_9_
  100.2 1.1 slab.1.a_ref
  101.3 3.0 %collective-permute-start.24 = (f32[96,128]{1,0:T(8,128)S(1)}, f32[96,128]{1,0:T(8,128)S(1)}, u32[]{:S(2)}, u32[]{:S(2)}) collective-permute-start(f32[96,128]{1,0:T(8,128)S(1)} %slab.1.a_ref), channel_id=1, source_target_pairs={{0,2},{1,3},{2,0},{3,1},{4,6},{5,7},{6,4},{7,5},{8,10},{9,11},{10,... | collective-permute-start | bytes 147464 | tf_op jit(solution)/shard_map/ppermute | solution.py:373
  104.7 2.3 %collective-permute-start.26 = (f32[96,128]{1,0:T(8,128)S(1)}, f32[96,128]{1,0:T(8,128)S(1)}, u32[]{:S(2)}, u32[]{:S(2)}) collective-permute-start(f32[96,128]{1,0:T(8,128)S(1)} %slab.1.a_ref), channel_id=1, source_target_pairs={{0,3},{1,0},{2,1},{3,2},{4,7},{5,4},{6,5},{7,6},{8,11},{9,8},{10,9... | collective-permute-start | bytes 147464 | tf_op jit(solution)/shard_map/ppermute | solution.py:373
  107.0 1.5 %collective-permute-done.25.c_ref = f32[96,128]{1,0:T(8,128)S(1)} collective-permute-done((f32[96,128]{1,0:T(8,128)S(1)}, f32[96,128]{1,0:T(8,128)S(1)}, u32[]{:S(2)}, u32[]{:S(2)}) %collective-permute-start.25) | collective-permute-done | bytes 49184 | tf_op jit(solution)/shard_map/ppermute | solution.py:373
  108.5 4.7 %solve.1 = (f32[137,1,137]{2,1,0:T(1,128)}, f32[1,137]{1,0:T(1,128)}, f32[1,137]{1,0:T(1,128)}) custom-call(f32[96,128]{1,0:T(8,128)S(1)} %slab.1.a_ref, f32[96,128]{1,0:T(8,128)S(1)} %collective-permute-done.24.b_ref, f32[96,128]{1,0:T(8,128)S(1)} %collective-permute-done.25.c_ref, f32[96,128]{1,0:T(8,128)S(1)} %collective-permute-done.26.d_ref), custom_call_target="tpu_custom_call" | custom-call | tf_op jit(solution)/shard_map/solve/pallas_call | solution.py:377
  (40 shorter events, 6.4 us)
Async XLA Ops:
  0.6 93.4 %copy-start = (f32[64,2176]{1,0:T(8,128)S(1)}, f32[64,2176]{1,0:T(8,128)}, u32[]{:S(2)}) copy-start(f32[64,2176]{1,0:T(8,128)} %param.8) | copy-start | bytes 1671172
  0.6 9.5 %copy-start.1 = (bf16[64,8,137]{2,1,0:T(8,128)(2,1)S(1)}, bf16[64,8,137]{2,1,0:T(8,128)(2,1)}, u32[]{:S(2)}) copy-start(bf16[64,8,137]{2,1,0:T(8,128)(2,1)} %st_ref.3) | copy-start | bytes 420868
  0.7 60.7 %copy-start.3 = (s32[64]{0:T(128)S(1)}, s32[64]{0:T(128)}, u32[]{:S(2)}) copy-start(s32[64]{0:T(128)} %param.9) | copy-start | bytes 772
  0.7 65.7 %copy-start.2 = (f32[2176]{0:T(1024)S(1)}, f32[2176]{0:T(1024)}, u32[]{:S(2)}) copy-start(f32[2176]{0:T(1024)} %param.7) | copy-start | bytes 26116
  3.7 21.9 %collective-permute-start = (bf16[3,8,2176]{2,1,0:T(8,128)(2,1)}, bf16[3,8,2176]{2,1,0:T(8,128)(2,1)S(1)}, u32[]{:S(2)}, u32[]{:S(2)}) collective-permute-start(bf16[3,8,2176]{2,1,0:T(8,128)(2,1)} %get-tuple-element.34), channel_id=1, source_target_pairs={{0,128},{4,132},{8,136},{12,140},{16,144},{20,148},{24,152},{28,15... | collective-permute-start | bytes 313352 | tf_op jit(solution)/shard_map/ppermute | solution.py:130
  7.3 19.6 %collective-permute-start.1 = (bf16[3,8,2176]{2,1,0:T(8,128)(2,1)}, bf16[3,8,2176]{2,1,0:T(8,128)(2,1)S(1)}, u32[]{:S(2)}, u32[]{:S(2)}) collective-permute-start(bf16[3,8,2176]{2,1,0:T(8,128)(2,1)} %get-tuple-element.35), channel_id=1, source_target_pairs={{0,132},{4,128},{8,140},{12,136},{16,148},{20,144},{24,156},{28,15... | collective-permute-start | bytes 313352 | tf_op jit(solution)/shard_map/ppermute | solution.py:130
  10.2 8.0 %collective-permute-start.14 = (bf16[9,8,128]{2,1,0:T(8,128)(2,1)S(1)}, bf16[9,8,128]{2,1,0:T(8,128)(2,1)S(1)}, u32[]{:S(2)}, u32[]{:S(2)}) collective-permute-start(bf16[9,8,128]{2,1,0:T(8,128)(2,1)S(1)} %get-tuple-element.49), channel_id=1, source_target_pairs={{0,32},{4,36},{8,40},{12,44},{16,48},{20,52},{24,56},{28,60},{32,0... | collective-permute-start | bytes 55304 | tf_op jit(solution)/shard_map/ppermute | solution.py:130
  15.5 14.5 %collective-permute-start.2 = (bf16[3,8,2176]{2,1,0:T(8,128)(2,1)}, bf16[3,8,2176]{2,1,0:T(8,128)(2,1)S(1)}, u32[]{:S(2)}, u32[]{:S(2)}) collective-permute-start(bf16[3,8,2176]{2,1,0:T(8,128)(2,1)} %get-tuple-element.36), channel_id=1, source_target_pairs={{0,64},{4,68},{8,72},{12,76},{16,80},{20,84},{24,88},{28,92},{32,9... | collective-permute-start | bytes 313352 | tf_op jit(solution)/shard_map/ppermute | solution.py:130
  16.7 13.3 %collective-permute-start.3 = (bf16[3,8,2176]{2,1,0:T(8,128)(2,1)}, bf16[3,8,2176]{2,1,0:T(8,128)(2,1)S(1)}, u32[]{:S(2)}, u32[]{:S(2)}) collective-permute-start(bf16[3,8,2176]{2,1,0:T(8,128)(2,1)} %get-tuple-element.37), channel_id=1, source_target_pairs={{0,192},{4,196},{8,200},{12,204},{16,208},{20,212},{24,216},{28,22... | collective-permute-start | bytes 313352 | tf_op jit(solution)/shard_map/ppermute | solution.py:130
  18.2 5.6 %collective-permute-start.15 = (bf16[9,8,128]{2,1,0:T(8,128)(2,1)S(1)}, bf16[9,8,128]{2,1,0:T(8,128)(2,1)S(1)}, u32[]{:S(2)}, u32[]{:S(2)}) collective-permute-start(bf16[9,8,128]{2,1,0:T(8,128)(2,1)S(1)} %get-tuple-element.50), channel_id=1, source_target_pairs={{0,24},{4,28},{8,32},{12,36},{16,40},{20,44},{24,48},{28,52},{32,5... | collective-permute-start | bytes 55304 | tf_op jit(solution)/shard_map/ppermute | solution.py:130
  23.8 8.9 %collective-permute-start.4 = (bf16[3,8,2176]{2,1,0:T(8,128)(2,1)}, bf16[3,8,2176]{2,1,0:T(8,128)(2,1)S(1)}, u32[]{:S(2)}, u32[]{:S(2)}) collective-permute-start(bf16[3,8,2176]{2,1,0:T(8,128)(2,1)} %get-tuple-element.38), channel_id=1, source_target_pairs={{0,68},{4,64},{8,76},{12,72},{16,84},{20,80},{24,92},{28,88},{32,1... | collective-permute-start | bytes 313352 | tf_op jit(solution)/shard_map/ppermute | solution.py:130
  25.6 30.3 %collective-permute-start.10 = (bf16[8,8,2432]{2,1,0:T(8,128)(2,1)}, bf16[8,8,2432]{2,1,0:T(8,128)(2,1)S(1)}, u32[]{:S(2)}, u32[]{:S(2)}) collective-permute-start(bf16[8,8,2432]{2,1,0:T(8,128)(2,1)} %get-tuple-element.44), channel_id=1, source_target_pairs={{0,16},{4,20},{8,24},{12,28},{16,32},{20,36},{24,40},{28,44},{32,4... | collective-permute-start | bytes 933896 | tf_op jit(solution)/shard_map/ppermute | solution.py:130
  26.9 31.3 %collective-permute-start.11 = (bf16[8,8,2432]{2,1,0:T(8,128)(2,1)}, bf16[8,8,2432]{2,1,0:T(8,128)(2,1)S(1)}, u32[]{:S(2)}, u32[]{:S(2)}) collective-permute-start(bf16[8,8,2432]{2,1,0:T(8,128)(2,1)} %get-tuple-element.45), channel_id=1, source_target_pairs={{0,48},{4,52},{8,56},{12,60},{16,0},{20,4},{24,8},{28,12},{32,16},... | collective-permute-start | bytes 933896 | tf_op jit(solution)/shard_map/ppermute | solution.py:130
  30.0 31.9 %collective-permute-start.12 = (bf16[8,8,2432]{2,1,0:T(8,128)(2,1)}, bf16[8,8,2432]{2,1,0:T(8,128)(2,1)S(1)}, u32[]{:S(2)}, u32[]{:S(2)}) collective-permute-start(bf16[8,8,2432]{2,1,0:T(8,128)(2,1)} %get-tuple-element.46), channel_id=1, source_target_pairs={{0,8},{4,12},{8,16},{12,20},{16,24},{20,28},{24,32},{28,36},{32,40... | collective-permute-start | bytes 933896 | tf_op jit(solution)/shard_map/ppermute | solution.py:130
  30.0 31.9 %collective-permute-start.13 = (bf16[8,8,2432]{2,1,0:T(8,128)(2,1)}, bf16[8,8,2432]{2,1,0:T(8,128)(2,1)S(1)}, u32[]{:S(2)}, u32[]{:S(2)}) collective-permute-start(bf16[8,8,2432]{2,1,0:T(8,128)(2,1)} %get-tuple-element.47), channel_id=1, source_target_pairs={{0,56},{4,60},{8,0},{12,4},{16,8},{20,12},{24,16},{28,20},{32,24},... | collective-permute-start | bytes 933896 | tf_op jit(solution)/shard_map/ppermute | solution.py:130
  32.7 5.4 %collective-permute-start.5 = (bf16[3,8,2176]{2,1,0:T(8,128)(2,1)}, bf16[3,8,2176]{2,1,0:T(8,128)(2,1)S(1)}, u32[]{:S(2)}, u32[]{:S(2)}) collective-permute-start(bf16[3,8,2176]{2,1,0:T(8,128)(2,1)} %get-tuple-element.39), channel_id=1, source_target_pairs={{0,196},{4,192},{8,204},{12,200},{16,212},{20,208},{24,220},{28,21... | collective-permute-start | bytes 313352 | tf_op jit(solution)/shard_map/ppermute | solution.py:130
  38.1 1.5 %collective-permute-start.6 = (bf16[3,8,2176]{2,1,0:T(8,128)(2,1)}, bf16[3,8,2176]{2,1,0:T(8,128)(2,1)S(1)}, u32[]{:S(2)}, u32[]{:S(2)}) collective-permute-start(bf16[3,8,2176]{2,1,0:T(8,128)(2,1)} %get-tuple-element.40), channel_id=1, source_target_pairs={{0,4},{4,0},{8,12},{12,8},{16,20},{20,16},{24,28},{28,24},{32,36},... | collective-permute-start | bytes 313352 | tf_op jit(solution)/shard_map/ppermute | solution.py:130
  39.7 13.1 %collective-permute-start.16 = (bf16[9,8,128]{2,1,0:T(8,128)(2,1)S(1)}, bf16[9,8,128]{2,1,0:T(8,128)(2,1)S(1)}, u32[]{:S(2)}, u32[]{:S(2)}) collective-permute-start(bf16[9,8,128]{2,1,0:T(8,128)(2,1)S(1)} %get-tuple-element.51), channel_id=1, source_target_pairs={{0,40},{4,44},{8,48},{12,52},{16,56},{20,60},{24,0},{28,4},{32,8},... | collective-permute-start | bytes 55304 | tf_op jit(solution)/shard_map/ppermute | solution.py:130
  52.8 14.2 %collective-permute-start.7 = (bf16[8,8,2176]{2,1,0:T(8,128)(2,1)}, bf16[8,8,2176]{2,1,0:T(8,128)(2,1)S(1)}, u32[]{:S(2)}, u32[]{:S(2)}) collective-permute-start(bf16[8,8,2176]{2,1,0:T(8,128)(2,1)} %get-tuple-element.41), channel_id=1, source_target_pairs={{0,32},{4,36},{8,40},{12,44},{16,48},{20,52},{24,56},{28,60},{32,0... | collective-permute-start | bytes 835592 | tf_op jit(solution)/shard_map/ppermute | solution.py:130
  55.9 32.7 %collective-permute-start.8 = (bf16[8,8,2176]{2,1,0:T(8,128)(2,1)}, bf16[8,8,2176]{2,1,0:T(8,128)(2,1)S(1)}, u32[]{:S(2)}, u32[]{:S(2)}) collective-permute-start(bf16[8,8,2176]{2,1,0:T(8,128)(2,1)} %get-tuple-element.42), channel_id=1, source_target_pairs={{0,24},{4,28},{8,32},{12,36},{16,40},{20,44},{24,48},{28,52},{32,5... | collective-permute-start | bytes 835592 | tf_op jit(solution)/shard_map/ppermute | solution.py:130
  58.2 32.0 %collective-permute-start.9 = (bf16[8,8,2176]{2,1,0:T(8,128)(2,1)S(1)}, bf16[8,8,2176]{2,1,0:T(8,128)(2,1)S(1)}, u32[]{:S(2)}, u32[]{:S(2)}) collective-permute-start(bf16[8,8,2176]{2,1,0:T(8,128)(2,1)S(1)} %get-tuple-element.43), channel_id=1, source_target_pairs={{0,40},{4,44},{8,48},{12,52},{16,56},{20,60},{24,0},{28,4},{32,8},... | collective-permute-start | bytes 835592 | tf_op jit(solution)/shard_map/ppermute | solution.py:130
  62.1 28.7 %collective-permute-start.17 = (bf16[5,8,2688]{2,1,0:T(8,128)(2,1)S(1)}, bf16[5,8,2688]{2,1,0:T(8,128)(2,1)S(1)}, u32[]{:S(2)}, u32[]{:S(2)}) collective-permute-start(bf16[5,8,2688]{2,1,0:T(8,128)(2,1)S(1)} %get-tuple-element.53), channel_id=1, source_target_pairs={{0,128},{4,132},{8,136},{12,140},{16,144},{20,148},{24,152},{28,15... | collective-permute-start | bytes 645128 | tf_op jit(solution)/shard_map/ppermute | solution.py:130
  64.6 28.6 %collective-permute-start.18 = (bf16[5,8,2688]{2,1,0:T(8,128)(2,1)S(1)}, bf16[5,8,2688]{2,1,0:T(8,128)(2,1)S(1)}, u32[]{:S(2)}, u32[]{:S(2)}) collective-permute-start(bf16[5,8,2688]{2,1,0:T(8,128)(2,1)S(1)} %get-tuple-element.54), channel_id=1, source_target_pairs={{0,132},{4,128},{8,140},{12,136},{16,148},{20,144},{24,156},{28,15... | collective-permute-start | bytes 645128 | tf_op jit(solution)/shard_map/ppermute | solution.py:130
  67.0 27.0 %collective-permute-start.19 = (bf16[5,8,2688]{2,1,0:T(8,128)(2,1)S(1)}, bf16[5,8,2688]{2,1,0:T(8,128)(2,1)S(1)}, u32[]{:S(2)}, u32[]{:S(2)}) collective-permute-start(bf16[5,8,2688]{2,1,0:T(8,128)(2,1)S(1)} %get-tuple-element.55), channel_id=1, source_target_pairs={{0,64},{4,68},{8,72},{12,76},{16,80},{20,84},{24,88},{28,92},{32,9... | collective-permute-start | bytes 645128 | tf_op jit(solution)/shard_map/ppermute | solution.py:130
  88.6 6.2 %collective-permute-start.20 = (bf16[5,8,2688]{2,1,0:T(8,128)(2,1)S(1)}, bf16[5,8,2688]{2,1,0:T(8,128)(2,1)S(1)}, u32[]{:S(2)}, u32[]{:S(2)}) collective-permute-start(bf16[5,8,2688]{2,1,0:T(8,128)(2,1)S(1)} %get-tuple-element.56), channel_id=1, source_target_pairs={{0,192},{4,196},{8,200},{12,204},{16,208},{20,212},{24,216},{28,22... | collective-permute-start | bytes 645128 | tf_op jit(solution)/shard_map/ppermute | solution.py:130
  90.2 8.9 %collective-permute-start.21 = (bf16[5,8,2688]{2,1,0:T(8,128)(2,1)S(1)}, bf16[5,8,2688]{2,1,0:T(8,128)(2,1)S(1)}, u32[]{:S(2)}, u32[]{:S(2)}) collective-permute-start(bf16[5,8,2688]{2,1,0:T(8,128)(2,1)S(1)} %get-tuple-element.57), channel_id=1, source_target_pairs={{0,68},{4,64},{8,76},{12,72},{16,84},{20,80},{24,92},{28,88},{32,1... | collective-permute-start | bytes 645128 | tf_op jit(solution)/shard_map/ppermute | solution.py:130
  90.8 9.4 %collective-permute-start.22 = (bf16[5,8,2688]{2,1,0:T(8,128)(2,1)S(1)}, bf16[5,8,2688]{2,1,0:T(8,128)(2,1)S(1)}, u32[]{:S(2)}, u32[]{:S(2)}) collective-permute-start(bf16[5,8,2688]{2,1,0:T(8,128)(2,1)S(1)} %get-tuple-element.58), channel_id=1, source_target_pairs={{0,196},{4,192},{8,204},{12,200},{16,212},{20,208},{24,220},{28,21... | collective-permute-start | bytes 645128 | tf_op jit(solution)/shard_map/ppermute | solution.py:130
  93.1 7.1 %collective-permute-start.23 = (bf16[5,8,2688]{2,1,0:T(8,128)(2,1)S(1)}, bf16[5,8,2688]{2,1,0:T(8,128)(2,1)S(1)}, u32[]{:S(2)}, u32[]{:S(2)}) collective-permute-start(bf16[5,8,2688]{2,1,0:T(8,128)(2,1)S(1)} %get-tuple-element.59), channel_id=1, source_target_pairs={{0,4},{4,0},{8,12},{12,8},{16,20},{20,16},{24,28},{28,24},{32,36},... | collective-permute-start | bytes 645128 | tf_op jit(solution)/shard_map/ppermute | solution.py:130
  101.3 5.7 %collective-permute-start.24 = (f32[96,128]{1,0:T(8,128)S(1)}, f32[96,128]{1,0:T(8,128)S(1)}, u32[]{:S(2)}, u32[]{:S(2)}) collective-permute-start(f32[96,128]{1,0:T(8,128)S(1)} %slab.1.a_ref), channel_id=1, source_target_pairs={{0,2},{1,3},{2,0},{3,1},{4,6},{5,7},{6,4},{7,5},{8,10},{9,11},{10,... | collective-permute-start | bytes 147464 | tf_op jit(solution)/shard_map/ppermute | solution.py:373
  104.3 4.2 %collective-permute-start.25 = (f32[96,128]{1,0:T(8,128)S(1)}, f32[96,128]{1,0:T(8,128)S(1)}, u32[]{:S(2)}, u32[]{:S(2)}) collective-permute-start(f32[96,128]{1,0:T(8,128)S(1)} %slab.1.a_ref), channel_id=1, source_target_pairs={{0,1},{1,2},{2,3},{3,0},{4,5},{5,6},{6,7},{7,4},{8,9},{9,10},{10,1... | collective-permute-start | bytes 147464 | tf_op jit(solution)/shard_map/ppermute | solution.py:373
  104.7 3.8 %collective-permute-start.26 = (f32[96,128]{1,0:T(8,128)S(1)}, f32[96,128]{1,0:T(8,128)S(1)}, u32[]{:S(2)}, u32[]{:S(2)}) collective-permute-start(f32[96,128]{1,0:T(8,128)S(1)} %slab.1.a_ref), channel_id=1, source_target_pairs={{0,3},{1,0},{2,1},{3,2},{4,7},{5,4},{6,5},{7,6},{8,11},{9,8},{10,9... | collective-permute-start | bytes 147464 | tf_op jit(solution)/shard_map/ppermute | solution.py:373
where the time goes:
time: 114 us; the launch traced here: 113 us
  starting transfers between devices  54.9 us (48%)
  waiting for transfers between devices  46.2 us (41%)
  Pallas kernels  9.99 us (9%)
    ppermute x24, starting transfers between devices, moved(): return lax.ppermute(a, 'mem', pairs)  49.3 us
    ppermute x24, waiting for transfers between devices, moved(): return lax.ppermute(a, 'mem', pairs)  44.8 us
    ppermute x3, starting transfers between devices, shards(): lax.ppermute(part, 'chan', [(j, (j + k) % chan) for j in range(chan)])  5.68 us
    pallas_call x1, Pallas kernels, shards(): pl.pallas_call(functools.partial(solve_kernel, states), out_shape=[jax.Sh...  4.69 us
    pallas_call x1, Pallas kernels, gathered(): pl.pallas_call(spread_kernel, out_shape=sent + [pltpu.VMEM(a.shape, a.dty...  3 us
  transfers between devices with their start and end apart: 27, of which 9 were waited for; matrix products, arithmetic and copies ran while one was open for 1% of the time, Pallas kernels for 1%

commit v1 on v0

--- a/solution.py
+++ b/solution.py
@@ -163,27 +163,43 @@
     swap_both = in_vmem(functools.partial(swap_both_kernel, st.shape[2]), both, len(NEAR) + len(FAR))
     near = swap_both(*near, *packed)
     near = [a if o == (0, 0) else moved(a, o[0], 0, o[1]) for a, o in zip(near, ACROSS)]
-    return far + near
-
-
-def slab_kernel(states, members_all, *refs):
-    parts, (weight_ref, innov_ref, out_ref, x_ref) = refs[:-4], refs[-4:]
-    width = weight_ref.shape[1]
-    far, near = parts[: len(FAR)], parts[len(FAR) :]
-    members = far[0].shape[1]
+    rows = members * len(ACROSS)
+    sums = in_vmem(
+        functools.partial(early_kernel, st.shape[2]),
+        [
+            jax.ShapeDtypeStruct((rows * len(FAR), 2 * LANES), rad.dtype),
+            jax.ShapeDtypeStruct((st.shape[2], width), jnp.float32),
+        ],
+        len(ACROSS),
+        scratch_shapes=[pltpu.VMEM((rows * len(NEAR), wide), rad.dtype)],
+    )(*near)
+    return list(far) + list(sums)
+
+
+def early_kernel(states, *refs):
+    near, (far_ref, cross_ref, x_ref) = refs[:-3], refs[-3:]
+    width = cross_ref.shape[1]
+    wide = x_ref.shape[1]
+    members = near[0].shape[1]
     block = members * len(NEAR)
-    above = members * len(ACROSS) * len(FAR)
-    for k, part in enumerate(far):
-        x_ref[k * members * len(ACROSS) : (k + 1) * members * len(ACROSS), 0:width] = part[...].reshape(-1, width)
     for o, part in enumerate(near):
-        x_ref[above + o * block : above + (o + 1) * block, :] = part[:, :, 0 : x_ref.shape[1]].reshape(block, -1)
+        x_ref[o * block : (o + 1) * block, :] = part[:, :, 0:wide].reshape(block, wide)
         for k in range(len(FAR)):
             row = (k * len(ACROSS) + o) * members
-            base = width + 2 * LANES
-            x_ref[row : row + members, width : width + states] = part[k, :, base : base + states]
-    rad = x_ref[:, 0:width]
+            far_ref[row : row + members, 0:states] = part[k, :, wide : wide + states]
+    tn = (((0,), (0,)), ((), ()))
     st = x_ref[:, width : width + states]
-    cross = lax.dot_general(st, rad, (((0,), (0,)), ((), ())), preferred_element_type=jnp.float32)
+    cross_ref[...] = lax.dot_general(st, x_ref[:, 0:width], tn, preferred_element_type=jnp.float32)
+
+
+def slab_kernel(states, members_all, *refs):
+    far, (states_ref, cross_ref, weight_ref, innov_ref, out_ref, x_ref) = refs[:-6], refs[-6:]
+    rows = far[0].shape[0] * far[0].shape[1]
+    for k, part in enumerate(far):
+        x_ref[k * rows : (k + 1) * rows, :] = part[...].reshape(rows, -1)
+    tn = (((0,), (0,)), ((), ()))
+    st = states_ref[:, 0:states]
+    cross = cross_ref[...] + lax.dot_general(st, x_ref[...], tn, preferred_element_type=jnp.float32)
     root = jnp.sqrt(weight_ref[...])
     y = cross * (root * (1.0 / (members_all - 1)))
     y1 = y.astype(jnp.bfloat16)
@@ -365,7 +381,7 @@
         out_shape=jax.ShapeDtypeStruct((PACKED, LANES), f32),
         in_specs=[pl.BlockSpec(memory_space=pltpu.VMEM)] * (len(blocks) + 2),
         out_specs=pl.BlockSpec(memory_space=pltpu.VMEM),
-        scratch_shapes=[pltpu.VMEM((members_all, slab_width + 2 * LANES), jnp.bfloat16)],
+        scratch_shapes=[pltpu.VMEM(blocks[-2].shape[:1] + (slab_width,), jnp.bfloat16)],
         compiler_params=pltpu.CompilerParams(vmem_limit_bytes=24 * 2**20),
         name="slab",
     )(*blocks, weight, innov)

time: 114 us -> 131 us (1.15)
  the two profiles are of different devices: /device:TPU:1 before, /device:TPU:56 now
where the time goes in v1:
time: 131 us
  waiting for transfers between devices  84.7 us (65%)
  starting transfers between devices  34.5 us (26%)
  Pallas kernels  9.54 us (7%)
    ppermute x24, waiting for transfers between devices, moved(): return lax.ppermute(a, 'mem', pairs)  79.4 us
    ppermute x24, starting transfers between devices, moved(): return lax.ppermute(a, 'mem', pairs)  31 us
    ppermute x3, waiting for transfers between devices, shards(): lax.ppermute(part, 'chan', [(j, (j + k) % chan) for j in range(chan)])  5.3 us
    pallas_call x1, Pallas kernels, shards(): pl.pallas_call(functools.partial(solve_kernel, states), out_shape=[jax.Sh...  4.69 us
    ppermute x3, starting transfers between devices, shards(): lax.ppermute(part, 'chan', [(j, (j + k) % chan) for j in range(chan)])  3.5 us
    pallas_call x1, Pallas kernels, gathered(): pl.pallas_call(spread_kernel, out_shape=sent + [pltpu.VMEM(a.shape, a.dty...  2.99 us
  transfers between devices with their start and end apart: 27, of which 15 were waited for; matrix products, arithmetic and copies ran while one was open for 1% of the time, Pallas kernels for 1%

profile of v1, /device:TPU:56, one launch (start us, length us, event | category | flops | bytes accessed | tf_op | source)
XLA Modules:
  0.0 131.0 jit_solution(16349151502495336882)
XLA Ops:
  0.7 3.0 %spread.1 = (bf16[8,8,2432]{2,1,0:T(8,128)(2,1)}, bf16[8,8,2432]{2,1,0:T(8,128)(2,1)}, bf16[8,8,2432]{2,1,0:T(8,128)(2,1)}, bf16[8,8,2432]{2,1,0:T(8,128)(2,1)},...) custom-call(bf16[64,8,2176]{2,1,0:T(8,128)(2,1)} %rad_ref.1, ...), custom_call_target="tpu_custom_call" | custom-call | tf_op jit(solution)/shard_map/spread/pallas_call | solution.py:140
  3.7 3.3 %collective-permute-start.10 = (bf16[8,8,2432]{2,1,0:T(8,128)(2,1)}, bf16[8,8,2432]{2,1,0:T(8,128)(2,1)S(1)}, u32[]{:S(2)}, u32[]{:S(2)}) collective-permute-start(bf16[8,8,2432]{2,1,0:T(8,128)(2,1)} %get-tuple-element.46), channel_id=1, source_target_pairs={{0,16},{4,20},{8,24},{12,28},{16,32},{20,36},{24,40},{28,44},{32,4... | collective-permute-start | bytes 933896 | tf_op jit(solution)/shard_map/ppermute | solution.py:130
  7.0 2.2 %collective-permute-start.11 = (bf16[8,8,2432]{2,1,0:T(8,128)(2,1)}, bf16[8,8,2432]{2,1,0:T(8,128)(2,1)S(1)}, u32[]{:S(2)}, u32[]{:S(2)}) collective-permute-start(bf16[8,8,2432]{2,1,0:T(8,128)(2,1)} %get-tuple-element.47), channel_id=1, source_target_pairs={{0,48},{4,52},{8,56},{12,60},{16,0},{20,4},{24,8},{28,12},{32,16},... | collective-permute-start | bytes 933896 | tf_op jit(solution)/shard_map/ppermute | solution.py:130
  9.2 0.9 collective-permute-start.12
  10.2 1.1 collective-permute-start.13
  11.4 5.0 %collective-permute-start.14 = (bf16[9,8,128]{2,1,0:T(8,128)(2,1)S(1)}, bf16[9,8,128]{2,1,0:T(8,128)(2,1)S(1)}, u32[]{:S(2)}, u32[]{:S(2)}) collective-permute-start(bf16[9,8,128]{2,1,0:T(8,128)(2,1)S(1)} %get-tuple-element.51), channel_id=1, source_target_pairs={{0,32},{4,36},{8,40},{12,44},{16,48},{20,52},{24,56},{28,60},{32,0... | collective-permute-start | bytes 55304 | tf_op jit(solution)/shard_map/ppermute | solution.py:130
  16.4 18.4 %collective-permute-done.14.refs_5_ = bf16[9,8,128]{2,1,0:T(8,128)(2,1)S(1)} collective-permute-done((bf16[9,8,128]{2,1,0:T(8,128)(2,1)S(1)}, bf16[9,8,128]{2,1,0:T(8,128)(2,1)S(1)}, u32[]{:S(2)}, u32[]{:S(2)}) %collective-permute-start.14) | collective-permute-done | bytes 18464 | tf_op jit(solution)/shard_map/ppermute | solution.py:130
  34.8 6.8 %collective-permute-done.15.refs_6_ = bf16[9,8,128]{2,1,0:T(8,128)(2,1)S(1)} collective-permute-done((bf16[9,8,128]{2,1,0:T(8,128)(2,1)S(1)}, bf16[9,8,128]{2,1,0:T(8,128)(2,1)S(1)}, u32[]{:S(2)}, u32[]{:S(2)}) %collective-permute-start.15) | collective-permute-done | bytes 18464 | tf_op jit(solution)/shard_map/ppermute | solution.py:130
  41.5 1.2 collective-permute-start.16
  42.8 5.5 %collective-permute-done.16.refs_7_ = bf16[9,8,128]{2,1,0:T(8,128)(2,1)S(1)} collective-permute-done((bf16[9,8,128]{2,1,0:T(8,128)(2,1)S(1)}, bf16[9,8,128]{2,1,0:T(8,128)(2,1)S(1)}, u32[]{:S(2)}, u32[]{:S(2)}) %collective-permute-start.16) | collective-permute-done | bytes 18464 | tf_op jit(solution)/shard_map/ppermute | solution.py:130
  48.3 3.0 %collective-permute-start = (bf16[3,8,2176]{2,1,0:T(8,128)(2,1)}, bf16[3,8,2176]{2,1,0:T(8,128)(2,1)S(1)}, u32[]{:S(2)}, u32[]{:S(2)}) collective-permute-start(bf16[3,8,2176]{2,1,0:T(8,128)(2,1)} %get-tuple-element.36), channel_id=1, source_target_pairs={{0,128},{4,132},{8,136},{12,140},{16,144},{20,148},{24,152},{28,15... | collective-permute-start | bytes 313352 | tf_op jit(solution)/shard_map/ppermute | solution.py:130
  51.3 3.4 %collective-permute-done.refs_1_ = bf16[3,8,2176]{2,1,0:T(8,128)(2,1)S(1)} collective-permute-done((bf16[3,8,2176]{2,1,0:T(8,128)(2,1)}, bf16[3,8,2176]{2,1,0:T(8,128)(2,1)S(1)}, u32[]{:S(2)}, u32[]{:S(2)}) %collective-permute-start) | collective-permute-done | bytes 104480 | tf_op jit(solution)/shard_map/ppermute | solution.py:130
  54.7 6.9 %collective-permute-done.1.refs_2_ = bf16[3,8,2176]{2,1,0:T(8,128)(2,1)S(1)} collective-permute-done((bf16[3,8,2176]{2,1,0:T(8,128)(2,1)}, bf16[3,8,2176]{2,1,0:T(8,128)(2,1)S(1)}, u32[]{:S(2)}, u32[]{:S(2)}) %collective-permute-start.1) | collective-permute-done | bytes 104480 | tf_op jit(solution)/shard_map/ppermute | solution.py:130
  62.3 2.5 %collective-permute-start.3 = (bf16[3,8,2176]{2,1,0:T(8,128)(2,1)}, bf16[3,8,2176]{2,1,0:T(8,128)(2,1)S(1)}, u32[]{:S(2)}, u32[]{:S(2)}) collective-permute-start(bf16[3,8,2176]{2,1,0:T(8,128)(2,1)} %get-tuple-element.39), channel_id=1, source_target_pairs={{0,192},{4,196},{8,200},{12,204},{16,208},{20,212},{24,216},{28,22... | collective-permute-start | bytes 313352 | tf_op jit(solution)/shard_map/ppermute | solution.py:130
  64.8 3.0 %collective-permute-start.5 = (bf16[3,8,2176]{2,1,0:T(8,128)(2,1)}, bf16[3,8,2176]{2,1,0:T(8,128)(2,1)S(1)}, u32[]{:S(2)}, u32[]{:S(2)}) collective-permute-start(bf16[3,8,2176]{2,1,0:T(8,128)(2,1)} %get-tuple-element.41), channel_id=1, source_target_pairs={{0,196},{4,192},{8,204},{12,200},{16,212},{20,208},{24,220},{28,21... | collective-permute-start | bytes 313352 | tf_op jit(solution)/shard_map/ppermute | solution.py:130
  68.7 3.3 %collective-permute-start.18 = (bf16[5,8,2688]{2,1,0:T(8,128)(2,1)S(1)}, bf16[5,8,2688]{2,1,0:T(8,128)(2,1)S(1)}, u32[]{:S(2)}, u32[]{:S(2)}) collective-permute-start(bf16[5,8,2688]{2,1,0:T(8,128)(2,1)S(1)} %get-tuple-element.56), channel_id=1, source_target_pairs={{0,132},{4,128},{8,140},{12,136},{16,148},{20,144},{24,156},{28,15... | collective-permute-start | bytes 645128 | tf_op jit(solution)/shard_map/ppermute | solution.py:130
  72.0 7.0 %collective-permute-done.5.refs_6_ = bf16[3,8,2176]{2,1,0:T(8,128)(2,1)S(1)} collective-permute-done((bf16[3,8,2176]{2,1,0:T(8,128)(2,1)}, bf16[3,8,2176]{2,1,0:T(8,128)(2,1)S(1)}, u32[]{:S(2)}, u32[]{:S(2)}) %collective-permute-start.5) | collective-permute-done | bytes 104480 | tf_op jit(solution)/shard_map/ppermute | solution.py:130
  79.8 1.7 %collective-permute-start.7 = (bf16[8,8,2176]{2,1,0:T(8,128)(2,1)S(1)}, bf16[8,8,2176]{2,1,0:T(8,128)(2,1)S(1)}, u32[]{:S(2)}, u32[]{:S(2)}) collective-permute-start(bf16[8,8,2176]{2,1,0:T(8,128)(2,1)S(1)} %get-tuple-element.43), channel_id=1, source_target_pairs={{0,32},{4,36},{8,40},{12,44},{16,48},{20,52},{24,56},{28,60},{32,0... | collective-permute-start | bytes 835592 | tf_op jit(solution)/shard_map/ppermute | solution.py:130
  82.1 5.0 %collective-permute-done.19.refs_3_ = bf16[5,8,2688]{2,1,0:T(8,128)(2,1)S(1)} collective-permute-done((bf16[5,8,2688]{2,1,0:T(8,128)(2,1)S(1)}, bf16[5,8,2688]{2,1,0:T(8,128)(2,1)S(1)}, u32[]{:S(2)}, u32[]{:S(2)}) %collective-permute-start.19) | collective-permute-done | bytes 215072 | tf_op jit(solution)/shard_map/ppermute | solution.py:130
  87.1 1.2 collective-permute-start.9
  88.8 2.8 %collective-permute-done.21.refs_5_ = bf16[5,8,2688]{2,1,0:T(8,128)(2,1)S(1)} collective-permute-done((bf16[5,8,2688]{2,1,0:T(8,128)(2,1)S(1)}, bf16[5,8,2688]{2,1,0:T(8,128)(2,1)S(1)}, u32[]{:S(2)}, u32[]{:S(2)}) %collective-permute-start.21) | collective-permute-done | bytes 215072 | tf_op jit(solution)/shard_map/ppermute | solution.py:130
  91.6 1.1 collective-permute-start.23
  92.8 2.5 %collective-permute-done.22.refs_6_ = bf16[5,8,2688]{2,1,0:T(8,128)(2,1)S(1)} collective-permute-done((bf16[5,8,2688]{2,1,0:T(8,128)(2,1)S(1)}, bf16[5,8,2688]{2,1,0:T(8,128)(2,1)S(1)}, u32[]{:S(2)}, u32[]{:S(2)}) %collective-permute-start.22) | collective-permute-done | bytes 215072 | tf_op jit(solution)/shard_map/ppermute | solution.py:130
  95.8 4.5 %collective-permute-done.7.refs_0_ = bf16[8,8,2176]{2,1,0:T(8,128)(2,1)S(1)} collective-permute-done((bf16[8,8,2176]{2,1,0:T(8,128)(2,1)S(1)}, bf16[8,8,2176]{2,1,0:T(8,128)(2,1)S(1)}, u32[]{:S(2)}, u32[]{:S(2)}) %collective-permute-start.7) | collective-permute-done | bytes 278560 | tf_op jit(solution)/shard_map/ppermute | solution.py:130
  100.3 12.2 %collective-permute-done.8.refs_1_ = bf16[8,8,2176]{2,1,0:T(8,128)(2,1)S(1)} collective-permute-done((bf16[8,8,2176]{2,1,0:T(8,128)(2,1)S(1)}, bf16[8,8,2176]{2,1,0:T(8,128)(2,1)S(1)}, u32[]{:S(2)}, u32[]{:S(2)}) %collective-permute-start.8) | collective-permute-done | bytes 278560 | tf_op jit(solution)/shard_map/ppermute | solution.py:130
  112.5 4.0 %collective-permute-done.9.refs_2_ = bf16[8,8,2176]{2,1,0:T(8,128)(2,1)S(1)} collective-permute-done((bf16[8,8,2176]{2,1,0:T(8,128)(2,1)S(1)}, bf16[8,8,2176]{2,1,0:T(8,128)(2,1)S(1)}, u32[]{:S(2)}, u32[]{:S(2)}) %collective-permute-start.9) | collective-permute-done | bytes 278560 | tf_op jit(solution)/shard_map/ppermute | solution.py:130
  116.5 0.9 slab.1.a_ref
  117.4 1.3 %collective-permute-start.24 = (f32[96,128]{1,0:T(8,128)S(1)}, f32[96,128]{1,0:T(8,128)S(1)}, u32[]{:S(2)}, u32[]{:S(2)}) collective-permute-start(f32[96,128]{1,0:T(8,128)S(1)} %slab.1.a_ref), channel_id=1, source_target_pairs={{0,2},{1,3},{2,0},{3,1},{4,6},{5,7},{6,4},{7,5},{8,10},{9,11},{10,... | collective-permute-start | bytes 147464 | tf_op jit(solution)/shard_map/ppermute | solution.py:389
  118.7 2.2 %collective-permute-start.25 = (f32[96,128]{1,0:T(8,128)S(1)}, f32[96,128]{1,0:T(8,128)S(1)}, u32[]{:S(2)}, u32[]{:S(2)}) collective-permute-start(f32[96,128]{1,0:T(8,128)S(1)} %slab.1.a_ref), channel_id=1, source_target_pairs={{0,1},{1,2},{2,3},{3,0},{4,5},{5,6},{6,7},{7,4},{8,9},{9,10},{10,1... | collective-permute-start | bytes 147464 | tf_op jit(solution)/shard_map/ppermute | solution.py:389
  120.9 2.2 %collective-permute-done.24.b_ref = f32[96,128]{1,0:T(8,128)S(1)} collective-permute-done((f32[96,128]{1,0:T(8,128)S(1)}, f32[96,128]{1,0:T(8,128)S(1)}, u32[]{:S(2)}, u32[]{:S(2)}) %collective-permute-start.24) | collective-permute-done | bytes 49184 | tf_op jit(solution)/shard_map/ppermute | solution.py:389
  123.1 3.1 %collective-permute-done.26.d_ref = f32[96,128]{1,0:T(8,128)S(1)} collective-permute-done((f32[96,128]{1,0:T(8,128)S(1)}, f32[96,128]{1,0:T(8,128)S(1)}, u32[]{:S(2)}, u32[]{:S(2)}) %collective-permute-start.26) | collective-permute-done | bytes 49184 | tf_op jit(solution)/shard_map/ppermute | solution.py:389
  126.2 4.7 %solve.1 = (f32[137,1,137]{2,1,0:T(1,128)}, f32[1,137]{1,0:T(1,128)}, f32[1,137]{1,0:T(1,128)}) custom-call(f32[96,128]{1,0:T(8,128)S(1)} %slab.1.a_ref, f32[96,128]{1,0:T(8,128)S(1)} %collective-permute-done.24.b_ref, f32[96,128]{1,0:T(8,128)S(1)} %collective-permute-done.25.c_ref, f32[96,128]{1,0:T(8,128)S(1)} %collective-permute-done.26.d_ref), custom_call_target="tpu_custom_call" | custom-call | tf_op jit(solution)/shard_map/solve/pallas_call | solution.py:393
  (41 shorter events, 4.2 us)
Async XLA Ops:
  0.6 92.1 %copy-start = (f32[64,2176]{1,0:T(8,128)S(1)}, f32[64,2176]{1,0:T(8,128)}, u32[]{:S(2)}) copy-start(f32[64,2176]{1,0:T(8,128)} %param.8) | copy-start | bytes 1671172
  0.6 10.6 %copy-start.1 = (bf16[64,8,137]{2,1,0:T(8,128)(2,1)S(1)}, bf16[64,8,137]{2,1,0:T(8,128)(2,1)}, u32[]{:S(2)}) copy-start(bf16[64,8,137]{2,1,0:T(8,128)(2,1)} %st_ref.3) | copy-start | bytes 420868
  0.7 67.1 %copy-start.3 = (s32[64]{0:T(128)S(1)}, s32[64]{0:T(128)}, u32[]{:S(2)}) copy-start(s32[64]{0:T(128)} %param.9) | copy-start | bytes 772
  0.7 78.3 %copy-start.2 = (f32[2176]{0:T(1024)S(1)}, f32[2176]{0:T(1024)}, u32[]{:S(2)}) copy-start(f32[2176]{0:T(1024)} %param.7) | copy-start | bytes 26116
  3.7 58.6 %collective-permute-start.10 = (bf16[8,8,2432]{2,1,0:T(8,128)(2,1)}, bf16[8,8,2432]{2,1,0:T(8,128)(2,1)S(1)}, u32[]{:S(2)}, u32[]{:S(2)}) collective-permute-start(bf16[8,8,2432]{2,1,0:T(8,128)(2,1)} %get-tuple-element.46), channel_id=1, source_target_pairs={{0,16},{4,20},{8,24},{12,28},{16,32},{20,36},{24,40},{28,44},{32,4... | collective-permute-start | bytes 933896 | tf_op jit(solution)/shard_map/ppermute | solution.py:130
  7.0 57.8 %collective-permute-start.11 = (bf16[8,8,2432]{2,1,0:T(8,128)(2,1)}, bf16[8,8,2432]{2,1,0:T(8,128)(2,1)S(1)}, u32[]{:S(2)}, u32[]{:S(2)}) collective-permute-start(bf16[8,8,2432]{2,1,0:T(8,128)(2,1)} %get-tuple-element.47), channel_id=1, source_target_pairs={{0,48},{4,52},{8,56},{12,60},{16,0},{20,4},{24,8},{28,12},{32,16},... | collective-permute-start | bytes 933896 | tf_op jit(solution)/shard_map/ppermute | solution.py:130
  9.2 55.6 %collective-permute-start.12 = (bf16[8,8,2432]{2,1,0:T(8,128)(2,1)}, bf16[8,8,2432]{2,1,0:T(8,128)(2,1)S(1)}, u32[]{:S(2)}, u32[]{:S(2)}) collective-permute-start(bf16[8,8,2432]{2,1,0:T(8,128)(2,1)} %get-tuple-element.48), channel_id=1, source_target_pairs={{0,8},{4,12},{8,16},{12,20},{16,24},{20,28},{24,32},{28,36},{32,40... | collective-permute-start | bytes 933896 | tf_op jit(solution)/shard_map/ppermute | solution.py:130
  10.2 57.6 %collective-permute-start.13 = (bf16[8,8,2432]{2,1,0:T(8,128)(2,1)}, bf16[8,8,2432]{2,1,0:T(8,128)(2,1)S(1)}, u32[]{:S(2)}, u32[]{:S(2)}) collective-permute-start(bf16[8,8,2432]{2,1,0:T(8,128)(2,1)} %get-tuple-element.49), channel_id=1, source_target_pairs={{0,56},{4,60},{8,0},{12,4},{16,8},{20,12},{24,16},{28,20},{32,24},... | collective-permute-start | bytes 933896 | tf_op jit(solution)/shard_map/ppermute | solution.py:130
  11.4 23.4 %collective-permute-start.14 = (bf16[9,8,128]{2,1,0:T(8,128)(2,1)S(1)}, bf16[9,8,128]{2,1,0:T(8,128)(2,1)S(1)}, u32[]{:S(2)}, u32[]{:S(2)}) collective-permute-start(bf16[9,8,128]{2,1,0:T(8,128)(2,1)S(1)} %get-tuple-element.51), channel_id=1, source_target_pairs={{0,32},{4,36},{8,40},{12,44},{16,48},{20,52},{24,56},{28,60},{32,0... | collective-permute-start | bytes 55304 | tf_op jit(solution)/shard_map/ppermute | solution.py:130
  34.8 6.8 %collective-permute-start.15 = (bf16[9,8,128]{2,1,0:T(8,128)(2,1)S(1)}, bf16[9,8,128]{2,1,0:T(8,128)(2,1)S(1)}, u32[]{:S(2)}, u32[]{:S(2)}) collective-permute-start(bf16[9,8,128]{2,1,0:T(8,128)(2,1)S(1)} %get-tuple-element.52), channel_id=1, source_target_pairs={{0,24},{4,28},{8,32},{12,36},{16,40},{20,44},{24,48},{28,52},{32,5... | collective-permute-start | bytes 55304 | tf_op jit(solution)/shard_map/ppermute | solution.py:130
  41.5 6.8 %collective-permute-start.16 = (bf16[9,8,128]{2,1,0:T(8,128)(2,1)S(1)}, bf16[9,8,128]{2,1,0:T(8,128)(2,1)S(1)}, u32[]{:S(2)}, u32[]{:S(2)}) collective-permute-start(bf16[9,8,128]{2,1,0:T(8,128)(2,1)S(1)} %get-tuple-element.53), channel_id=1, source_target_pairs={{0,40},{4,44},{8,48},{12,52},{16,56},{20,60},{24,0},{28,4},{32,8},... | collective-permute-start | bytes 55304 | tf_op jit(solution)/shard_map/ppermute | solution.py:130
  48.3 6.4 %collective-permute-start = (bf16[3,8,2176]{2,1,0:T(8,128)(2,1)}, bf16[3,8,2176]{2,1,0:T(8,128)(2,1)S(1)}, u32[]{:S(2)}, u32[]{:S(2)}) collective-permute-start(bf16[3,8,2176]{2,1,0:T(8,128)(2,1)} %get-tuple-element.36), channel_id=1, source_target_pairs={{0,128},{4,132},{8,136},{12,140},{16,144},{20,148},{24,152},{28,15... | collective-permute-start | bytes 313352 | tf_op jit(solution)/shard_map/ppermute | solution.py:130
  54.7 6.9 %collective-permute-start.1 = (bf16[3,8,2176]{2,1,0:T(8,128)(2,1)}, bf16[3,8,2176]{2,1,0:T(8,128)(2,1)S(1)}, u32[]{:S(2)}, u32[]{:S(2)}) collective-permute-start(bf16[3,8,2176]{2,1,0:T(8,128)(2,1)} %get-tuple-element.37), channel_id=1, source_target_pairs={{0,132},{4,128},{8,140},{12,136},{16,148},{20,144},{24,156},{28,15... | collective-permute-start | bytes 313352 | tf_op jit(solution)/shard_map/ppermute | solution.py:130
  61.6 7.0 %collective-permute-start.2 = (bf16[3,8,2176]{2,1,0:T(8,128)(2,1)}, bf16[3,8,2176]{2,1,0:T(8,128)(2,1)S(1)}, u32[]{:S(2)}, u32[]{:S(2)}) collective-permute-start(bf16[3,8,2176]{2,1,0:T(8,128)(2,1)} %get-tuple-element.38), channel_id=1, source_target_pairs={{0,64},{4,68},{8,72},{12,76},{16,80},{20,84},{24,88},{28,92},{32,9... | collective-permute-start | bytes 313352 | tf_op jit(solution)/shard_map/ppermute | solution.py:130
  62.3 6.4 %collective-permute-start.3 = (bf16[3,8,2176]{2,1,0:T(8,128)(2,1)}, bf16[3,8,2176]{2,1,0:T(8,128)(2,1)S(1)}, u32[]{:S(2)}, u32[]{:S(2)}) collective-permute-start(bf16[3,8,2176]{2,1,0:T(8,128)(2,1)} %get-tuple-element.39), channel_id=1, source_target_pairs={{0,192},{4,196},{8,200},{12,204},{16,208},{20,212},{24,216},{28,22... | collective-permute-start | bytes 313352 | tf_op jit(solution)/shard_map/ppermute | solution.py:130
  64.8 7.2 %collective-permute-start.4 = (bf16[3,8,2176]{2,1,0:T(8,128)(2,1)}, bf16[3,8,2176]{2,1,0:T(8,128)(2,1)S(1)}, u32[]{:S(2)}, u32[]{:S(2)}) collective-permute-start(bf16[3,8,2176]{2,1,0:T(8,128)(2,1)} %get-tuple-element.40), channel_id=1, source_target_pairs={{0,68},{4,64},{8,76},{12,72},{16,84},{20,80},{24,92},{28,88},{32,1... | collective-permute-start | bytes 313352 | tf_op jit(solution)/shard_map/ppermute | solution.py:130
  64.8 14.2 %collective-permute-start.5 = (bf16[3,8,2176]{2,1,0:T(8,128)(2,1)}, bf16[3,8,2176]{2,1,0:T(8,128)(2,1)S(1)}, u32[]{:S(2)}, u32[]{:S(2)}) collective-permute-start(bf16[3,8,2176]{2,1,0:T(8,128)(2,1)} %get-tuple-element.41), channel_id=1, source_target_pairs={{0,196},{4,192},{8,204},{12,200},{16,212},{20,208},{24,220},{28,21... | collective-permute-start | bytes 313352 | tf_op jit(solution)/shard_map/ppermute | solution.py:130
  67.8 11.2 %collective-permute-start.6 = (bf16[3,8,2176]{2,1,0:T(8,128)(2,1)}, bf16[3,8,2176]{2,1,0:T(8,128)(2,1)S(1)}, u32[]{:S(2)}, u32[]{:S(2)}) collective-permute-start(bf16[3,8,2176]{2,1,0:T(8,128)(2,1)} %get-tuple-element.42), channel_id=1, source_target_pairs={{0,4},{4,0},{8,12},{12,8},{16,20},{20,16},{24,28},{28,24},{32,36},... | collective-permute-start | bytes 313352 | tf_op jit(solution)/shard_map/ppermute | solution.py:130
  68.6 11.2 %collective-permute-start.17 = (bf16[5,8,2688]{2,1,0:T(8,128)(2,1)S(1)}, bf16[5,8,2688]{2,1,0:T(8,128)(2,1)S(1)}, u32[]{:S(2)}, u32[]{:S(2)}) collective-permute-start(bf16[5,8,2688]{2,1,0:T(8,128)(2,1)S(1)} %get-tuple-element.55), channel_id=1, source_target_pairs={{0,128},{4,132},{8,136},{12,140},{16,144},{20,148},{24,152},{28,15... | collective-permute-start | bytes 645128 | tf_op jit(solution)/shard_map/ppermute | solution.py:130
  68.7 13.4 %collective-permute-start.18 = (bf16[5,8,2688]{2,1,0:T(8,128)(2,1)S(1)}, bf16[5,8,2688]{2,1,0:T(8,128)(2,1)S(1)}, u32[]{:S(2)}, u32[]{:S(2)}) collective-permute-start(bf16[5,8,2688]{2,1,0:T(8,128)(2,1)S(1)} %get-tuple-element.56), channel_id=1, source_target_pairs={{0,132},{4,128},{8,140},{12,136},{16,148},{20,144},{24,156},{28,15... | collective-permute-start | bytes 645128 | tf_op jit(solution)/shard_map/ppermute | solution.py:130
  72.0 15.1 %collective-permute-start.19 = (bf16[5,8,2688]{2,1,0:T(8,128)(2,1)S(1)}, bf16[5,8,2688]{2,1,0:T(8,128)(2,1)S(1)}, u32[]{:S(2)}, u32[]{:S(2)}) collective-permute-start(bf16[5,8,2688]{2,1,0:T(8,128)(2,1)S(1)} %get-tuple-element.57), channel_id=1, source_target_pairs={{0,64},{4,68},{8,72},{12,76},{16,80},{20,84},{24,88},{28,92},{32,9... | collective-permute-start | bytes 645128 | tf_op jit(solution)/shard_map/ppermute | solution.py:130
  79.0 9.4 %collective-permute-start.20 = (bf16[5,8,2688]{2,1,0:T(8,128)(2,1)S(1)}, bf16[5,8,2688]{2,1,0:T(8,128)(2,1)S(1)}, u32[]{:S(2)}, u32[]{:S(2)}) collective-permute-start(bf16[5,8,2688]{2,1,0:T(8,128)(2,1)S(1)} %get-tuple-element.58), channel_id=1, source_target_pairs={{0,192},{4,196},{8,200},{12,204},{16,208},{20,212},{24,216},{28,22... | collective-permute-start | bytes 645128 | tf_op jit(solution)/shard_map/ppermute | solution.py:130
  79.0 12.6 %collective-permute-start.21 = (bf16[5,8,2688]{2,1,0:T(8,128)(2,1)S(1)}, bf16[5,8,2688]{2,1,0:T(8,128)(2,1)S(1)}, u32[]{:S(2)}, u32[]{:S(2)}) collective-permute-start(bf16[5,8,2688]{2,1,0:T(8,128)(2,1)S(1)} %get-tuple-element.59), channel_id=1, source_target_pairs={{0,68},{4,64},{8,76},{12,72},{16,84},{20,80},{24,92},{28,88},{32,1... | collective-permute-start | bytes 645128 | tf_op jit(solution)/shard_map/ppermute | solution.py:130
  79.8 20.5 %collective-permute-start.7 = (bf16[8,8,2176]{2,1,0:T(8,128)(2,1)S(1)}, bf16[8,8,2176]{2,1,0:T(8,128)(2,1)S(1)}, u32[]{:S(2)}, u32[]{:S(2)}) collective-permute-start(bf16[8,8,2176]{2,1,0:T(8,128)(2,1)S(1)} %get-tuple-element.43), channel_id=1, source_target_pairs={{0,32},{4,36},{8,40},{12,44},{16,48},{20,52},{24,56},{28,60},{32,0... | collective-permute-start | bytes 835592 | tf_op jit(solution)/shard_map/ppermute | solution.py:130
  82.1 30.4 %collective-permute-start.8 = (bf16[8,8,2176]{2,1,0:T(8,128)(2,1)S(1)}, bf16[8,8,2176]{2,1,0:T(8,128)(2,1)S(1)}, u32[]{:S(2)}, u32[]{:S(2)}) collective-permute-start(bf16[8,8,2176]{2,1,0:T(8,128)(2,1)S(1)} %get-tuple-element.44), channel_id=1, source_target_pairs={{0,24},{4,28},{8,32},{12,36},{16,40},{20,44},{24,48},{28,52},{32,5... | collective-permute-start | bytes 835592 | tf_op jit(solution)/shard_map/ppermute | solution.py:130
  87.1 29.3 %collective-permute-start.9 = (bf16[8,8,2176]{2,1,0:T(8,128)(2,1)S(1)}, bf16[8,8,2176]{2,1,0:T(8,128)(2,1)S(1)}, u32[]{:S(2)}, u32[]{:S(2)}) collective-permute-start(bf16[8,8,2176]{2,1,0:T(8,128)(2,1)S(1)} %get-tuple-element.45), channel_id=1, source_target_pairs={{0,40},{4,44},{8,48},{12,52},{16,56},{20,60},{24,0},{28,4},{32,8},... | collective-permute-start | bytes 835592 | tf_op jit(solution)/shard_map/ppermute | solution.py:130
  88.4 6.8 %collective-permute-start.22 = (bf16[5,8,2688]{2,1,0:T(8,128)(2,1)S(1)}, bf16[5,8,2688]{2,1,0:T(8,128)(2,1)S(1)}, u32[]{:S(2)}, u32[]{:S(2)}) collective-permute-start(bf16[5,8,2688]{2,1,0:T(8,128)(2,1)S(1)} %get-tuple-element.60), channel_id=1, source_target_pairs={{0,196},{4,192},{8,204},{12,200},{16,212},{20,208},{24,220},{28,21... | collective-permute-start | bytes 645128 | tf_op jit(solution)/shard_map/ppermute | solution.py:130
  91.6 3.6 %collective-permute-start.23 = (bf16[5,8,2688]{2,1,0:T(8,128)(2,1)S(1)}, bf16[5,8,2688]{2,1,0:T(8,128)(2,1)S(1)}, u32[]{:S(2)}, u32[]{:S(2)}) collective-permute-start(bf16[5,8,2688]{2,1,0:T(8,128)(2,1)S(1)} %get-tuple-element.61), channel_id=1, source_target_pairs={{0,4},{4,0},{8,12},{12,8},{16,20},{20,16},{24,28},{28,24},{32,36},... | collective-permute-start | bytes 645128 | tf_op jit(solution)/shard_map/ppermute | solution.py:130
  117.4 5.7 %collective-permute-start.24 = (f32[96,128]{1,0:T(8,128)S(1)}, f32[96,128]{1,0:T(8,128)S(1)}, u32[]{:S(2)}, u32[]{:S(2)}) collective-permute-start(f32[96,128]{1,0:T(8,128)S(1)} %slab.1.a_ref), channel_id=1, source_target_pairs={{0,2},{1,3},{2,0},{3,1},{4,6},{5,7},{6,4},{7,5},{8,10},{9,11},{10,... | collective-permute-start | bytes 147464 | tf_op jit(solution)/shard_map/ppermute | solution.py:389
  118.7 4.4 %collective-permute-start.25 = (f32[96,128]{1,0:T(8,128)S(1)}, f32[96,128]{1,0:T(8,128)S(1)}, u32[]{:S(2)}, u32[]{:S(2)}) collective-permute-start(f32[96,128]{1,0:T(8,128)S(1)} %slab.1.a_ref), channel_id=1, source_target_pairs={{0,1},{1,2},{2,3},{3,0},{4,5},{5,6},{6,7},{7,4},{8,9},{9,10},{10,1... | collective-permute-start | bytes 147464 | tf_op jit(solution)/shard_map/ppermute | solution.py:389
  120.9 5.3 %collective-permute-start.26 = (f32[96,128]{1,0:T(8,128)S(1)}, f32[96,128]{1,0:T(8,128)S(1)}, u32[]{:S(2)}, u32[]{:S(2)}) collective-permute-start(f32[96,128]{1,0:T(8,128)S(1)} %slab.1.a_ref), channel_id=1, source_target_pairs={{0,3},{1,0},{2,1},{3,2},{4,7},{5,4},{6,5},{7,6},{8,11},{9,8},{10,9... | collective-permute-start | bytes 147464 | tf_op jit(solution)/shard_map/ppermute | solution.py:389

commit v2 on v1

--- a/solution.py
+++ b/solution.py
@@ -8,8 +8,8 @@
 from jax.sharding import PartitionSpec as P
 
 LANES = 128
-TOL = 2e-5
-FIRST_STEPS = 11
+TOL = 3e-5
+FIRST_STEPS = 10
 MORE_STEPS = 6
 MORE_ROUNDS = 8
 PACKED = 96
@@ -88,11 +88,11 @@
         out[len(ACROSS)] = jnp.concatenate(ends, axis=1).astype(out.dtype)
 
 
-def swap_kernel(many, *refs):
+def swap_kernel(many, start, *refs):
     come, go = refs[:many], refs[many:]
     for i, ref in enumerate(come):
         for j, out in enumerate(go):
-            out[i] = ref[j]
+            out[i] = ref[start + j]
 
 
 def swap_both_kernel(states, *refs):
@@ -157,8 +157,11 @@
     far = [a if o == (0, 0) else moved(a, o[0], 0, o[1]) for a, o in zip(far, ACROSS)]
     packed = in_vmem(pack_kernel, shape(len(ACROSS) + 1, LANES) * len(FAR), 1)(st)
     packed = [moved(a, 0, dz, 0) for a, dz in zip(packed, FAR)]
-    far = in_vmem(functools.partial(swap_kernel, len(ACROSS)), tall * len(FAR), len(ACROSS))(*far)
-    far = [moved(a, 0, dz, 0) for a, dz in zip(far, FAR)]
+    lead = in_vmem(functools.partial(swap_kernel, len(ACROSS), 0), tall, len(ACROSS))(*far)
+    lead = [moved(lead[0], 0, FAR[0], 0)]
+    rest = tall * (len(FAR) - 1)
+    rest = in_vmem(functools.partial(swap_kernel, len(ACROSS), 1), rest, len(ACROSS))(*far)
+    far = lead + [moved(a, 0, dz, 0) for a, dz in zip(rest, FAR[1:])]
     both = shape(len(NEAR), wide + 2 * LANES) * len(ACROSS)
     swap_both = in_vmem(functools.partial(swap_both_kernel, st.shape[2]), both, len(NEAR) + len(FAR))
     near = swap_both(*near, *packed)

time: 131 us -> 131 us (level)
  no operation moved by 1% of the time
where the time goes in v2:
time: 131 us
  waiting for transfers between devices  84.7 us (65%)
  starting transfers between devices  34.6 us (26%)
  Pallas kernels  9.39 us (7%)
    ppermute x24, waiting for transfers between devices, moved(): return lax.ppermute(a, 'mem', pairs)  79.4 us
    ppermute x24, starting transfers between devices, moved(): return lax.ppermute(a, 'mem', pairs)  31.1 us
    ppermute x3, waiting for transfers between devices, shards(): lax.ppermute(part, 'chan', [(j, (j + k) % chan) for j in range(chan)])  5.3 us
    pallas_call x1, Pallas kernels, shards(): pl.pallas_call(functools.partial(solve_kernel, states), out_shape=[jax.Sh...  4.54 us
    ppermute x3, starting transfers between devices, shards(): lax.ppermute(part, 'chan', [(j, (j + k) % chan) for j in range(chan)])  3.5 us
    pallas_call x1, Pallas kernels, gathered(): pl.pallas_call(spread_kernel, out_shape=sent + [pltpu.VMEM(a.shape, a.dty...  2.99 us
  transfers between devices with their start and end apart: 27, of which 15 were waited for; matrix products, arithmetic and copies ran while one was open for 1% of the time, Pallas kernels for 1%

profile of v2, /device:TPU:56, one launch (start us, length us, event | category | flops | bytes accessed | tf_op | source)
XLA Modules:
  0.0 130.9 jit_solution(827945286387162346)
XLA Ops:
  0.7 3.0 %spread.1 = (bf16[8,8,2432]{2,1,0:T(8,128)(2,1)}, bf16[8,8,2432]{2,1,0:T(8,128)(2,1)}, bf16[8,8,2432]{2,1,0:T(8,128)(2,1)}, bf16[8,8,2432]{2,1,0:T(8,128)(2,1)},...) custom-call(bf16[64,8,2176]{2,1,0:T(8,128)(2,1)} %rad_ref.1, ...), custom_call_target="tpu_custom_call" | custom-call | tf_op jit(solution)/shard_map/spread/pallas_call | solution.py:140
  3.7 3.3 %collective-permute-start.10 = (bf16[8,8,2432]{2,1,0:T(8,128)(2,1)}, bf16[8,8,2432]{2,1,0:T(8,128)(2,1)S(1)}, u32[]{:S(2)}, u32[]{:S(2)}) collective-permute-start(bf16[8,8,2432]{2,1,0:T(8,128)(2,1)} %get-tuple-element.44), channel_id=1, source_target_pairs={{0,16},{4,20},{8,24},{12,28},{16,32},{20,36},{24,40},{28,44},{32,4... | collective-permute-start | bytes 933896 | tf_op jit(solution)/shard_map/ppermute | solution.py:130
  7.0 2.2 %collective-permute-start.11 = (bf16[8,8,2432]{2,1,0:T(8,128)(2,1)}, bf16[8,8,2432]{2,1,0:T(8,128)(2,1)S(1)}, u32[]{:S(2)}, u32[]{:S(2)}) collective-permute-start(bf16[8,8,2432]{2,1,0:T(8,128)(2,1)} %get-tuple-element.45), channel_id=1, source_target_pairs={{0,48},{4,52},{8,56},{12,60},{16,0},{20,4},{24,8},{28,12},{32,16},... | collective-permute-start | bytes 933896 | tf_op jit(solution)/shard_map/ppermute | solution.py:130
  9.2 0.9 collective-permute-start.12
  10.2 1.1 collective-permute-start.13
  11.4 5.0 %collective-permute-start.14 = (bf16[9,8,128]{2,1,0:T(8,128)(2,1)S(1)}, bf16[9,8,128]{2,1,0:T(8,128)(2,1)S(1)}, u32[]{:S(2)}, u32[]{:S(2)}) collective-permute-start(bf16[9,8,128]{2,1,0:T(8,128)(2,1)S(1)} %get-tuple-element.49), channel_id=1, source_target_pairs={{0,32},{4,36},{8,40},{12,44},{16,48},{20,52},{24,56},{28,60},{32,0... | collective-permute-start | bytes 55304 | tf_op jit(solution)/shard_map/ppermute | solution.py:130
  16.4 18.4 %collective-permute-done.14.refs_5_ = bf16[9,8,128]{2,1,0:T(8,128)(2,1)S(1)} collective-permute-done((bf16[9,8,128]{2,1,0:T(8,128)(2,1)S(1)}, bf16[9,8,128]{2,1,0:T(8,128)(2,1)S(1)}, u32[]{:S(2)}, u32[]{:S(2)}) %collective-permute-start.14) | collective-permute-done | bytes 18464 | tf_op jit(solution)/shard_map/ppermute | solution.py:130
  34.8 6.8 %collective-permute-done.15.refs_6_ = bf16[9,8,128]{2,1,0:T(8,128)(2,1)S(1)} collective-permute-done((bf16[9,8,128]{2,1,0:T(8,128)(2,1)S(1)}, bf16[9,8,128]{2,1,0:T(8,128)(2,1)S(1)}, u32[]{:S(2)}, u32[]{:S(2)}) %collective-permute-start.15) | collective-permute-done | bytes 18464 | tf_op jit(solution)/shard_map/ppermute | solution.py:130
  41.5 1.2 collective-permute-start.16
  42.8 5.5 %collective-permute-done.16.refs_7_ = bf16[9,8,128]{2,1,0:T(8,128)(2,1)S(1)} collective-permute-done((bf16[9,8,128]{2,1,0:T(8,128)(2,1)S(1)}, bf16[9,8,128]{2,1,0:T(8,128)(2,1)S(1)}, u32[]{:S(2)}, u32[]{:S(2)}) %collective-permute-start.16) | collective-permute-done | bytes 18464 | tf_op jit(solution)/shard_map/ppermute | solution.py:130
  48.3 3.0 %collective-permute-start = (bf16[3,8,2176]{2,1,0:T(8,128)(2,1)}, bf16[3,8,2176]{2,1,0:T(8,128)(2,1)S(1)}, u32[]{:S(2)}, u32[]{:S(2)}) collective-permute-start(bf16[3,8,2176]{2,1,0:T(8,128)(2,1)} %get-tuple-element.35), channel_id=1, source_target_pairs={{0,128},{4,132},{8,136},{12,140},{16,144},{20,148},{24,152},{28,15... | collective-permute-start | bytes 313352 | tf_op jit(solution)/shard_map/ppermute | solution.py:130
  51.3 3.4 %collective-permute-done.refs_1_ = bf16[3,8,2176]{2,1,0:T(8,128)(2,1)S(1)} collective-permute-done((bf16[3,8,2176]{2,1,0:T(8,128)(2,1)}, bf16[3,8,2176]{2,1,0:T(8,128)(2,1)S(1)}, u32[]{:S(2)}, u32[]{:S(2)}) %collective-permute-start) | collective-permute-done | bytes 104480 | tf_op jit(solution)/shard_map/ppermute | solution.py:130
  54.7 6.9 %collective-permute-done.1.refs_2_ = bf16[3,8,2176]{2,1,0:T(8,128)(2,1)S(1)} collective-permute-done((bf16[3,8,2176]{2,1,0:T(8,128)(2,1)}, bf16[3,8,2176]{2,1,0:T(8,128)(2,1)S(1)}, u32[]{:S(2)}, u32[]{:S(2)}) %collective-permute-start.1) | collective-permute-done | bytes 104480 | tf_op jit(solution)/shard_map/ppermute | solution.py:130
  62.3 2.5 %collective-permute-start.3 = (bf16[3,8,2176]{2,1,0:T(8,128)(2,1)}, bf16[3,8,2176]{2,1,0:T(8,128)(2,1)S(1)}, u32[]{:S(2)}, u32[]{:S(2)}) collective-permute-start(bf16[3,8,2176]{2,1,0:T(8,128)(2,1)} %get-tuple-element.38), channel_id=1, source_target_pairs={{0,192},{4,196},{8,200},{12,204},{16,208},{20,212},{24,216},{28,22... | collective-permute-start | bytes 313352 | tf_op jit(solution)/shard_map/ppermute | solution.py:130
  64.8 3.0 %collective-permute-start.5 = (bf16[3,8,2176]{2,1,0:T(8,128)(2,1)}, bf16[3,8,2176]{2,1,0:T(8,128)(2,1)S(1)}, u32[]{:S(2)}, u32[]{:S(2)}) collective-permute-start(bf16[3,8,2176]{2,1,0:T(8,128)(2,1)} %get-tuple-element.40), channel_id=1, source_target_pairs={{0,196},{4,192},{8,204},{12,200},{16,212},{20,208},{24,220},{28,21... | collective-permute-start | bytes 313352 | tf_op jit(solution)/shard_map/ppermute | solution.py:130
  68.7 3.3 %collective-permute-start.18 = (bf16[5,8,2688]{2,1,0:T(8,128)(2,1)S(1)}, bf16[5,8,2688]{2,1,0:T(8,128)(2,1)S(1)}, u32[]{:S(2)}, u32[]{:S(2)}) collective-permute-start(bf16[5,8,2688]{2,1,0:T(8,128)(2,1)S(1)} %get-tuple-element.54), channel_id=1, source_target_pairs={{0,132},{4,128},{8,140},{12,136},{16,148},{20,144},{24,156},{28,15... | collective-permute-start | bytes 645128 | tf_op jit(solution)/shard_map/ppermute | solution.py:130
  72.0 7.0 %collective-permute-done.5.refs_6_ = bf16[3,8,2176]{2,1,0:T(8,128)(2,1)S(1)} collective-permute-done((bf16[3,8,2176]{2,1,0:T(8,128)(2,1)}, bf16[3,8,2176]{2,1,0:T(8,128)(2,1)S(1)}, u32[]{:S(2)}, u32[]{:S(2)}) %collective-permute-start.5) | collective-permute-done | bytes 104480 | tf_op jit(solution)/shard_map/ppermute | solution.py:130
  79.8 1.7 %collective-permute-start.7 = (bf16[8,8,2176]{2,1,0:T(8,128)(2,1)S(1)}, bf16[8,8,2176]{2,1,0:T(8,128)(2,1)S(1)}, u32[]{:S(2)}, u32[]{:S(2)}) collective-permute-start(bf16[8,8,2176]{2,1,0:T(8,128)(2,1)S(1)} %shard_map.76), channel_id=1, source_target_pairs={{0,32},{4,36},{8,40},{12,44},{16,48},{20,52},{24,56},{28,60},{32,0... | collective-permute-start | bytes 835592 | tf_op jit(solution)/shard_map/ppermute | solution.py:130
  82.1 5.0 %collective-permute-done.19.refs_3_ = bf16[5,8,2688]{2,1,0:T(8,128)(2,1)S(1)} collective-permute-done((bf16[5,8,2688]{2,1,0:T(8,128)(2,1)S(1)}, bf16[5,8,2688]{2,1,0:T(8,128)(2,1)S(1)}, u32[]{:S(2)}, u32[]{:S(2)}) %collective-permute-start.19) | collective-permute-done | bytes 215072 | tf_op jit(solution)/shard_map/ppermute | solution.py:130
  87.1 1.2 collective-permute-start.9
  88.9 2.8 %collective-permute-done.21.refs_5_ = bf16[5,8,2688]{2,1,0:T(8,128)(2,1)S(1)} collective-permute-done((bf16[5,8,2688]{2,1,0:T(8,128)(2,1)S(1)}, bf16[5,8,2688]{2,1,0:T(8,128)(2,1)S(1)}, u32[]{:S(2)}, u32[]{:S(2)}) %collective-permute-start.21) | collective-permute-done | bytes 215072 | tf_op jit(solution)/shard_map/ppermute | solution.py:130
  91.6 1.1 collective-permute-start.23
  92.8 2.4 %collective-permute-done.22.refs_6_ = bf16[5,8,2688]{2,1,0:T(8,128)(2,1)S(1)} collective-permute-done((bf16[5,8,2688]{2,1,0:T(8,128)(2,1)S(1)}, bf16[5,8,2688]{2,1,0:T(8,128)(2,1)S(1)}, u32[]{:S(2)}, u32[]{:S(2)}) %collective-permute-start.22) | collective-permute-done | bytes 215072 | tf_op jit(solution)/shard_map/ppermute | solution.py:130
  95.8 4.5 %collective-permute-done.7.refs_0_ = bf16[8,8,2176]{2,1,0:T(8,128)(2,1)S(1)} collective-permute-done((bf16[8,8,2176]{2,1,0:T(8,128)(2,1)S(1)}, bf16[8,8,2176]{2,1,0:T(8,128)(2,1)S(1)}, u32[]{:S(2)}, u32[]{:S(2)}) %collective-permute-start.7) | collective-permute-done | bytes 278560 | tf_op jit(solution)/shard_map/ppermute | solution.py:130
  100.3 12.2 %collective-permute-done.8.refs_1_ = bf16[8,8,2176]{2,1,0:T(8,128)(2,1)S(1)} collective-permute-done((bf16[8,8,2176]{2,1,0:T(8,128)(2,1)S(1)}, bf16[8,8,2176]{2,1,0:T(8,128)(2,1)S(1)}, u32[]{:S(2)}, u32[]{:S(2)}) %collective-permute-start.8) | collective-permute-done | bytes 278560 | tf_op jit(solution)/shard_map/ppermute | solution.py:130
  112.5 4.0 %collective-permute-done.9.refs_2_ = bf16[8,8,2176]{2,1,0:T(8,128)(2,1)S(1)} collective-permute-done((bf16[8,8,2176]{2,1,0:T(8,128)(2,1)S(1)}, bf16[8,8,2176]{2,1,0:T(8,128)(2,1)S(1)}, u32[]{:S(2)}, u32[]{:S(2)}) %collective-permute-start.9) | collective-permute-done | bytes 278560 | tf_op jit(solution)/shard_map/ppermute | solution.py:130
  116.5 0.9 slab.1.a_ref
  117.4 1.3 %collective-permute-start.24 = (f32[96,128]{1,0:T(8,128)S(1)}, f32[96,128]{1,0:T(8,128)S(1)}, u32[]{:S(2)}, u32[]{:S(2)}) collective-permute-start(f32[96,128]{1,0:T(8,128)S(1)} %slab.1.a_ref), channel_id=1, source_target_pairs={{0,2},{1,3},{2,0},{3,1},{4,6},{5,7},{6,4},{7,5},{8,10},{9,11},{10,... | collective-permute-start | bytes 147464 | tf_op jit(solution)/shard_map/ppermute | solution.py:392
  118.7 2.2 %collective-permute-start.25 = (f32[96,128]{1,0:T(8,128)S(1)}, f32[96,128]{1,0:T(8,128)S(1)}, u32[]{:S(2)}, u32[]{:S(2)}) collective-permute-start(f32[96,128]{1,0:T(8,128)S(1)} %slab.1.a_ref), channel_id=1, source_target_pairs={{0,1},{1,2},{2,3},{3,0},{4,5},{5,6},{6,7},{7,4},{8,9},{9,10},{10,1... | collective-permute-start | bytes 147464 | tf_op jit(solution)/shard_map/ppermute | solution.py:392
  120.9 2.2 %collective-permute-done.24.b_ref = f32[96,128]{1,0:T(8,128)S(1)} collective-permute-done((f32[96,128]{1,0:T(8,128)S(1)}, f32[96,128]{1,0:T(8,128)S(1)}, u32[]{:S(2)}, u32[]{:S(2)}) %collective-permute-start.24) | collective-permute-done | bytes 49184 | tf_op jit(solution)/shard_map/ppermute | solution.py:392
  123.1 3.1 %collective-permute-done.26.d_ref = f32[96,128]{1,0:T(8,128)S(1)} collective-permute-done((f32[96,128]{1,0:T(8,128)S(1)}, f32[96,128]{1,0:T(8,128)S(1)}, u32[]{:S(2)}, u32[]{:S(2)}) %collective-permute-start.26) | collective-permute-done | bytes 49184 | tf_op jit(solution)/shard_map/ppermute | solution.py:392
  126.2 4.5 %solve.1 = (f32[137,1,137]{2,1,0:T(1,128)}, f32[1,137]{1,0:T(1,128)}, f32[1,137]{1,0:T(1,128)}) custom-call(f32[96,128]{1,0:T(8,128)S(1)} %slab.1.a_ref, f32[96,128]{1,0:T(8,128)S(1)} %collective-permute-done.24.b_ref, f32[96,128]{1,0:T(8,128)S(1)} %collective-permute-done.25.c_ref, f32[96,128]{1,0:T(8,128)S(1)} %collective-permute-done.26.d_ref), custom_call_target="tpu_custom_call" | custom-call | tf_op jit(solution)/shard_map/solve/pallas_call | solution.py:396
  (42 shorter events, 4.2 us)
Async XLA Ops:
  0.6 92.1 %copy-start = (f32[64,2176]{1,0:T(8,128)S(1)}, f32[64,2176]{1,0:T(8,128)}, u32[]{:S(2)}) copy-start(f32[64,2176]{1,0:T(8,128)} %param.8) | copy-start | bytes 1671172
  0.6 10.6 %copy-start.1 = (bf16[64,8,137]{2,1,0:T(8,128)(2,1)S(1)}, bf16[64,8,137]{2,1,0:T(8,128)(2,1)}, u32[]{:S(2)}) copy-start(bf16[64,8,137]{2,1,0:T(8,128)(2,1)} %st_ref.3) | copy-start | bytes 420868
  0.7 67.1 %copy-start.3 = (s32[64]{0:T(128)S(1)}, s32[64]{0:T(128)}, u32[]{:S(2)}) copy-start(s32[64]{0:T(128)} %param.9) | copy-start | bytes 772
  0.7 78.3 %copy-start.2 = (f32[2176]{0:T(1024)S(1)}, f32[2176]{0:T(1024)}, u32[]{:S(2)}) copy-start(f32[2176]{0:T(1024)} %param.7) | copy-start | bytes 26116
  3.7 58.6 %collective-permute-start.10 = (bf16[8,8,2432]{2,1,0:T(8,128)(2,1)}, bf16[8,8,2432]{2,1,0:T(8,128)(2,1)S(1)}, u32[]{:S(2)}, u32[]{:S(2)}) collective-permute-start(bf16[8,8,2432]{2,1,0:T(8,128)(2,1)} %get-tuple-element.44), channel_id=1, source_target_pairs={{0,16},{4,20},{8,24},{12,28},{16,32},{20,36},{24,40},{28,44},{32,4... | collective-permute-start | bytes 933896 | tf_op jit(solution)/shard_map/ppermute | solution.py:130
  7.0 57.8 %collective-permute-start.11 = (bf16[8,8,2432]{2,1,0:T(8,128)(2,1)}, bf16[8,8,2432]{2,1,0:T(8,128)(2,1)S(1)}, u32[]{:S(2)}, u32[]{:S(2)}) collective-permute-start(bf16[8,8,2432]{2,1,0:T(8,128)(2,1)} %get-tuple-element.45), channel_id=1, source_target_pairs={{0,48},{4,52},{8,56},{12,60},{16,0},{20,4},{24,8},{28,12},{32,16},... | collective-permute-start | bytes 933896 | tf_op jit(solution)/shard_map/ppermute | solution.py:130
  9.2 55.6 %collective-permute-start.12 = (bf16[8,8,2432]{2,1,0:T(8,128)(2,1)}, bf16[8,8,2432]{2,1,0:T(8,128)(2,1)S(1)}, u32[]{:S(2)}, u32[]{:S(2)}) collective-permute-start(bf16[8,8,2432]{2,1,0:T(8,128)(2,1)} %get-tuple-element.46), channel_id=1, source_target_pairs={{0,8},{4,12},{8,16},{12,20},{16,24},{20,28},{24,32},{28,36},{32,40... | collective-permute-start | bytes 933896 | tf_op jit(solution)/shard_map/ppermute | solution.py:130
  10.2 57.6 %collective-permute-start.13 = (bf16[8,8,2432]{2,1,0:T(8,128)(2,1)}, bf16[8,8,2432]{2,1,0:T(8,128)(2,1)S(1)}, u32[]{:S(2)}, u32[]{:S(2)}) collective-permute-start(bf16[8,8,2432]{2,1,0:T(8,128)(2,1)} %get-tuple-element.47), channel_id=1, source_target_pairs={{0,56},{4,60},{8,0},{12,4},{16,8},{20,12},{24,16},{28,20},{32,24},... | collective-permute-start | bytes 933896 | tf_op jit(solution)/shard_map/ppermute | solution.py:130
  11.4 23.4 %collective-permute-start.14 = (bf16[9,8,128]{2,1,0:T(8,128)(2,1)S(1)}, bf16[9,8,128]{2,1,0:T(8,128)(2,1)S(1)}, u32[]{:S(2)}, u32[]{:S(2)}) collective-permute-start(bf16[9,8,128]{2,1,0:T(8,128)(2,1)S(1)} %get-tuple-element.49), channel_id=1, source_target_pairs={{0,32},{4,36},{8,40},{12,44},{16,48},{20,52},{24,56},{28,60},{32,0... | collective-permute-start | bytes 55304 | tf_op jit(solution)/shard_map/ppermute | solution.py:130
  34.8 6.8 %collective-permute-start.15 = (bf16[9,8,128]{2,1,0:T(8,128)(2,1)S(1)}, bf16[9,8,128]{2,1,0:T(8,128)(2,1)S(1)}, u32[]{:S(2)}, u32[]{:S(2)}) collective-permute-start(bf16[9,8,128]{2,1,0:T(8,128)(2,1)S(1)} %get-tuple-element.50), channel_id=1, source_target_pairs={{0,24},{4,28},{8,32},{12,36},{16,40},{20,44},{24,48},{28,52},{32,5... | collective-permute-start | bytes 55304 | tf_op jit(solution)/shard_map/ppermute | solution.py:130
  41.5 6.8 %collective-permute-start.16 = (bf16[9,8,128]{2,1,0:T(8,128)(2,1)S(1)}, bf16[9,8,128]{2,1,0:T(8,128)(2,1)S(1)}, u32[]{:S(2)}, u32[]{:S(2)}) collective-permute-start(bf16[9,8,128]{2,1,0:T(8,128)(2,1)S(1)} %get-tuple-element.51), channel_id=1, source_target_pairs={{0,40},{4,44},{8,48},{12,52},{16,56},{20,60},{24,0},{28,4},{32,8},... | collective-permute-start | bytes 55304 | tf_op jit(solution)/shard_map/ppermute | solution.py:130
  48.3 6.4 %collective-permute-start = (bf16[3,8,2176]{2,1,0:T(8,128)(2,1)}, bf16[3,8,2176]{2,1,0:T(8,128)(2,1)S(1)}, u32[]{:S(2)}, u32[]{:S(2)}) collective-permute-start(bf16[3,8,2176]{2,1,0:T(8,128)(2,1)} %get-tuple-element.35), channel_id=1, source_target_pairs={{0,128},{4,132},{8,136},{12,140},{16,144},{20,148},{24,152},{28,15... | collective-permute-start | bytes 313352 | tf_op jit(solution)/shard_map/ppermute | solution.py:130
  54.7 6.9 %collective-permute-start.1 = (bf16[3,8,2176]{2,1,0:T(8,128)(2,1)}, bf16[3,8,2176]{2,1,0:T(8,128)(2,1)S(1)}, u32[]{:S(2)}, u32[]{:S(2)}) collective-permute-start(bf16[3,8,2176]{2,1,0:T(8,128)(2,1)} %get-tuple-element.36), channel_id=1, source_target_pairs={{0,132},{4,128},{8,140},{12,136},{16,148},{20,144},{24,156},{28,15... | collective-permute-start | bytes 313352 | tf_op jit(solution)/shard_map/ppermute | solution.py:130
  61.6 7.0 %collective-permute-start.2 = (bf16[3,8,2176]{2,1,0:T(8,128)(2,1)}, bf16[3,8,2176]{2,1,0:T(8,128)(2,1)S(1)}, u32[]{:S(2)}, u32[]{:S(2)}) collective-permute-start(bf16[3,8,2176]{2,1,0:T(8,128)(2,1)} %get-tuple-element.37), channel_id=1, source_target_pairs={{0,64},{4,68},{8,72},{12,76},{16,80},{20,84},{24,88},{28,92},{32,9... | collective-permute-start | bytes 313352 | tf_op jit(solution)/shard_map/ppermute | solution.py:130
  62.3 6.4 %collective-permute-start.3 = (bf16[3,8,2176]{2,1,0:T(8,128)(2,1)}, bf16[3,8,2176]{2,1,0:T(8,128)(2,1)S(1)}, u32[]{:S(2)}, u32[]{:S(2)}) collective-permute-start(bf16[3,8,2176]{2,1,0:T(8,128)(2,1)} %get-tuple-element.38), channel_id=1, source_target_pairs={{0,192},{4,196},{8,200},{12,204},{16,208},{20,212},{24,216},{28,22... | collective-permute-start | bytes 313352 | tf_op jit(solution)/shard_map/ppermute | solution.py:130
  64.8 7.2 %collective-permute-start.4 = (bf16[3,8,2176]{2,1,0:T(8,128)(2,1)}, bf16[3,8,2176]{2,1,0:T(8,128)(2,1)S(1)}, u32[]{:S(2)}, u32[]{:S(2)}) collective-permute-start(bf16[3,8,2176]{2,1,0:T(8,128)(2,1)} %get-tuple-element.39), channel_id=1, source_target_pairs={{0,68},{4,64},{8,76},{12,72},{16,84},{20,80},{24,92},{28,88},{32,1... | collective-permute-start | bytes 313352 | tf_op jit(solution)/shard_map/ppermute | solution.py:130
  64.8 14.2 %collective-permute-start.5 = (bf16[3,8,2176]{2,1,0:T(8,128)(2,1)}, bf16[3,8,2176]{2,1,0:T(8,128)(2,1)S(1)}, u32[]{:S(2)}, u32[]{:S(2)}) collective-permute-start(bf16[3,8,2176]{2,1,0:T(8,128)(2,1)} %get-tuple-element.40), channel_id=1, source_target_pairs={{0,196},{4,192},{8,204},{12,200},{16,212},{20,208},{24,220},{28,21... | collective-permute-start | bytes 313352 | tf_op jit(solution)/shard_map/ppermute | solution.py:130
  67.8 11.2 %collective-permute-start.6 = (bf16[3,8,2176]{2,1,0:T(8,128)(2,1)}, bf16[3,8,2176]{2,1,0:T(8,128)(2,1)S(1)}, u32[]{:S(2)}, u32[]{:S(2)}) collective-permute-start(bf16[3,8,2176]{2,1,0:T(8,128)(2,1)} %get-tuple-element.41), channel_id=1, source_target_pairs={{0,4},{4,0},{8,12},{12,8},{16,20},{20,16},{24,28},{28,24},{32,36},... | collective-permute-start | bytes 313352 | tf_op jit(solution)/shard_map/ppermute | solution.py:130
  68.6 11.2 %collective-permute-start.17 = (bf16[5,8,2688]{2,1,0:T(8,128)(2,1)S(1)}, bf16[5,8,2688]{2,1,0:T(8,128)(2,1)S(1)}, u32[]{:S(2)}, u32[]{:S(2)}) collective-permute-start(bf16[5,8,2688]{2,1,0:T(8,128)(2,1)S(1)} %get-tuple-element.53), channel_id=1, source_target_pairs={{0,128},{4,132},{8,136},{12,140},{16,144},{20,148},{24,152},{28,15... | collective-permute-start | bytes 645128 | tf_op jit(solution)/shard_map/ppermute | solution.py:130
  68.7 13.4 %collective-permute-start.18 = (bf16[5,8,2688]{2,1,0:T(8,128)(2,1)S(1)}, bf16[5,8,2688]{2,1,0:T(8,128)(2,1)S(1)}, u32[]{:S(2)}, u32[]{:S(2)}) collective-permute-start(bf16[5,8,2688]{2,1,0:T(8,128)(2,1)S(1)} %get-tuple-element.54), channel_id=1, source_target_pairs={{0,132},{4,128},{8,140},{12,136},{16,148},{20,144},{24,156},{28,15... | collective-permute-start | bytes 645128 | tf_op jit(solution)/shard_map/ppermute | solution.py:130
  72.0 15.1 %collective-permute-start.19 = (bf16[5,8,2688]{2,1,0:T(8,128)(2,1)S(1)}, bf16[5,8,2688]{2,1,0:T(8,128)(2,1)S(1)}, u32[]{:S(2)}, u32[]{:S(2)}) collective-permute-start(bf16[5,8,2688]{2,1,0:T(8,128)(2,1)S(1)} %get-tuple-element.55), channel_id=1, source_target_pairs={{0,64},{4,68},{8,72},{12,76},{16,80},{20,84},{24,88},{28,92},{32,9... | collective-permute-start | bytes 645128 | tf_op jit(solution)/shard_map/ppermute | solution.py:130
  79.0 9.4 %collective-permute-start.20 = (bf16[5,8,2688]{2,1,0:T(8,128)(2,1)S(1)}, bf16[5,8,2688]{2,1,0:T(8,128)(2,1)S(1)}, u32[]{:S(2)}, u32[]{:S(2)}) collective-permute-start(bf16[5,8,2688]{2,1,0:T(8,128)(2,1)S(1)} %get-tuple-element.56), channel_id=1, source_target_pairs={{0,192},{4,196},{8,200},{12,204},{16,208},{20,212},{24,216},{28,22... | collective-permute-start | bytes 645128 | tf_op jit(solution)/shard_map/ppermute | solution.py:130
  79.0 12.6 %collective-permute-start.21 = (bf16[5,8,2688]{2,1,0:T(8,128)(2,1)S(1)}, bf16[5,8,2688]{2,1,0:T(8,128)(2,1)S(1)}, u32[]{:S(2)}, u32[]{:S(2)}) collective-permute-start(bf16[5,8,2688]{2,1,0:T(8,128)(2,1)S(1)} %get-tuple-element.57), channel_id=1, source_target_pairs={{0,68},{4,64},{8,76},{12,72},{16,84},{20,80},{24,92},{28,88},{32,1... | collective-permute-start | bytes 645128 | tf_op jit(solution)/shard_map/ppermute | solution.py:130
  79.8 20.5 %collective-permute-start.7 = (bf16[8,8,2176]{2,1,0:T(8,128)(2,1)S(1)}, bf16[8,8,2176]{2,1,0:T(8,128)(2,1)S(1)}, u32[]{:S(2)}, u32[]{:S(2)}) collective-permute-start(bf16[8,8,2176]{2,1,0:T(8,128)(2,1)S(1)} %shard_map.76), channel_id=1, source_target_pairs={{0,32},{4,36},{8,40},{12,44},{16,48},{20,52},{24,56},{28,60},{32,0... | collective-permute-start | bytes 835592 | tf_op jit(solution)/shard_map/ppermute | solution.py:130
  82.1 30.4 %collective-permute-start.8 = (bf16[8,8,2176]{2,1,0:T(8,128)(2,1)S(1)}, bf16[8,8,2176]{2,1,0:T(8,128)(2,1)S(1)}, u32[]{:S(2)}, u32[]{:S(2)}) collective-permute-start(bf16[8,8,2176]{2,1,0:T(8,128)(2,1)S(1)} %get-tuple-element.42), channel_id=1, source_target_pairs={{0,24},{4,28},{8,32},{12,36},{16,40},{20,44},{24,48},{28,52},{32,5... | collective-permute-start | bytes 835592 | tf_op jit(solution)/shard_map/ppermute | solution.py:130
  87.1 29.3 %collective-permute-start.9 = (bf16[8,8,2176]{2,1,0:T(8,128)(2,1)S(1)}, bf16[8,8,2176]{2,1,0:T(8,128)(2,1)S(1)}, u32[]{:S(2)}, u32[]{:S(2)}) collective-permute-start(bf16[8,8,2176]{2,1,0:T(8,128)(2,1)S(1)} %get-tuple-element.43), channel_id=1, source_target_pairs={{0,40},{4,44},{8,48},{12,52},{16,56},{20,60},{24,0},{28,4},{32,8},... | collective-permute-start | bytes 835592 | tf_op jit(solution)/shard_map/ppermute | solution.py:130
  88.4 6.8 %collective-permute-start.22 = (bf16[5,8,2688]{2,1,0:T(8,128)(2,1)S(1)}, bf16[5,8,2688]{2,1,0:T(8,128)(2,1)S(1)}, u32[]{:S(2)}, u32[]{:S(2)}) collective-permute-start(bf16[5,8,2688]{2,1,0:T(8,128)(2,1)S(1)} %get-tuple-element.58), channel_id=1, source_target_pairs={{0,196},{4,192},{8,204},{12,200},{16,212},{20,208},{24,220},{28,21... | collective-permute-start | bytes 645128 | tf_op jit(solution)/shard_map/ppermute | solution.py:130
  91.6 3.6 %collective-permute-start.23 = (bf16[5,8,2688]{2,1,0:T(8,128)(2,1)S(1)}, bf16[5,8,2688]{2,1,0:T(8,128)(2,1)S(1)}, u32[]{:S(2)}, u32[]{:S(2)}) collective-permute-start(bf16[5,8,2688]{2,1,0:T(8,128)(2,1)S(1)} %get-tuple-element.59), channel_id=1, source_target_pairs={{0,4},{4,0},{8,12},{12,8},{16,20},{20,16},{24,28},{28,24},{32,36},... | collective-permute-start | bytes 645128 | tf_op jit(solution)/shard_map/ppermute | solution.py:130
  117.4 5.7 %collective-permute-start.24 = (f32[96,128]{1,0:T(8,128)S(1)}, f32[96,128]{1,0:T(8,128)S(1)}, u32[]{:S(2)}, u32[]{:S(2)}) collective-permute-start(f32[96,128]{1,0:T(8,128)S(1)} %slab.1.a_ref), channel_id=1, source_target_pairs={{0,2},{1,3},{2,0},{3,1},{4,6},{5,7},{6,4},{7,5},{8,10},{9,11},{10,... | collective-permute-start | bytes 147464 | tf_op jit(solution)/shard_map/ppermute | solution.py:392
  118.7 4.4 %collective-permute-start.25 = (f32[96,128]{1,0:T(8,128)S(1)}, f32[96,128]{1,0:T(8,128)S(1)}, u32[]{:S(2)}, u32[]{:S(2)}) collective-permute-start(f32[96,128]{1,0:T(8,128)S(1)} %slab.1.a_ref), channel_id=1, source_target_pairs={{0,1},{1,2},{2,3},{3,0},{4,5},{5,6},{6,7},{7,4},{8,9},{9,10},{10,1... | collective-permute-start | bytes 147464 | tf_op jit(solution)/shard_map/ppermute | solution.py:392
  120.9 5.3 %collective-permute-start.26 = (f32[96,128]{1,0:T(8,128)S(1)}, f32[96,128]{1,0:T(8,128)S(1)}, u32[]{:S(2)}, u32[]{:S(2)}) collective-permute-start(f32[96,128]{1,0:T(8,128)S(1)} %slab.1.a_ref), channel_id=1, source_target_pairs={{0,3},{1,0},{2,1},{3,2},{4,7},{5,4},{6,5},{7,6},{8,11},{9,8},{10,9... | collective-permute-start | bytes 147464 | tf_op jit(solution)/shard_map/ppermute | solution.py:392
